TPU v7x, 32 devices: a whole 2x2x4 slice. The times are simulated.
32 devices in a mesh: dp: 8 (over z, x), rep: 4 (over y, core).
Axes of the slice: x: 2, y: 2, z: 4, core: 2. Of those that a mesh axis runs over, the one named last changes fastest.
Arguments:
- hot_ids: int32 [8192, 2], P(('dp', 'rep')), may hold values from 0 to 1023
- cold_owner: int32 [16384, 1], P(('dp', 'rep')), may hold values from 0 to 7; in each aligned block of 512 rows (0 to 511, 512 to 1023, ...) at most 128 rows name the same one
- cold_offset: int32 [16384], P(('dp', 'rep')), may hold values from 0 to 511
- labels: int32 [8192], P(('dp', 'rep')), may hold values 0 or 1
- top_weight: bfloat16 [512, 1024], replicated, may hold values from -0.25 to 0.25
- out_weight: float32 [1024], replicated, may hold values from -0.5 to 0.5
- cold_table: float32 [4096, 128], P('dp'), may hold values from -6 to 6
- cold_accum: float32 [4096, 128], P('dp'), may hold values from 0.0001 to 0.01
- hot_cache: float32 [1024, 128], replicated, may hold values from -6 to 6
- hot_accum: float32 [1024, 128], replicated, may hold values from 0.01 to 1
- pending: float32 [32768, 128], P(('dp', 'rep')), may hold values from -0.3 to 0.3
- refresh_blocks: int32 [3], replicated, may hold values from 0 to 7, as said below
- block_clock: int32 [8], replicated, may hold values from 0 to 8
Outputs:
- cold_table_new: float32 [4096, 128], P('dp')
- cold_accum_new: float32 [4096, 128], P('dp')
- hot_cache_new: float32 [1024, 128], replicated
- hot_accum_new: float32 [1024, 128], replicated
- pending_new: float32 [32768, 128], P(('dp', 'rep'))
- top_grad: float32 [512, 1024], P(('dp', 'rep'))
- out_grad: float32 [1024], replicated
Inputs may be any that keep to these rules, and one draw needn't show every extreme that they name: `cold_owner`: within the lookups of one device (512 rows), no owner is named more than 128 times. `refresh_blocks`: the block numbers are distinct.
All inputs are finite; a program needn't handle non-finite values. No bound on the sum of `labels` on one device may be relied on, other than what follows from the above.
Results may differ from a plain program's by a relative error of at most 0.00165.
The roundings to bfloat16 on the way count: a program that leaves them out, or rounds other values in their place, can miss the bound.
Values may be sent and summed in bfloat16 or wider, within the bound.
A program may use at most 64 MiB of HBM per device.

v0:
```python
import functools

import jax
import jax.numpy as jnp
from jax import lax
from jax.experimental import pallas as pl
from jax.experimental.pallas import tpu as pltpu
from jax.sharding import PartitionSpec as P

BLOCK = 128
MESH = pl.DeviceIdType.MESH


step_size = 0.5
epsilon = 1e-08


def adagrad(table_rows, accum_rows, gradient):
    accum_next = accum_rows + gradient * gradient
    return (table_rows - step_size * gradient / (jnp.sqrt(accum_next) + epsilon), accum_next)


def bit_of(index, weight):
    return lax.rem(lax.div(index, weight), 2)


def flipped(index, weight):
    return index + weight * (1 - 2 * bit_of(index, weight))


def greet(devices):
    barrier = pltpu.get_barrier_semaphore()
    for device in devices:
        pl.semaphore_signal(barrier, inc=1, device_id=device, device_id_type=MESH)
    pl.semaphore_wait(barrier, len(devices))


def chosen(offsets, rows):
    shape = (rows, offsets.shape[1])
    asks = lax.broadcasted_iota(jnp.int32, shape, 0) == jnp.broadcast_to(offsets, shape)
    return jnp.where(asks, 1.0, 0.0).astype(jnp.bfloat16)


def fetch_kernel(n, requests, table, asked_out, returned_out, asked, found, returned, sems):
    me, rep = lax.axis_index("dp"), lax.axis_index("rep")
    peers = [lax.rem(me + j, n) for j in range(1, n)]
    sources = [lax.rem(me + n - j, n) for j in range(1, n)]
    greet([(peer, rep) for peer in peers])
    asking = []
    for j, peer in enumerate(peers):
        copy = pltpu.make_async_remote_copy(
            requests.at[peer], asked.at[me], sems.at[0, j], sems.at[1, j], (peer, rep), MESH
        )
        copy.start()
        asking.append(copy)
    rows = table[...].astype(jnp.bfloat16)

    def rows_of(offsets):
        return lax.dot_general(
            chosen(offsets, rows.shape[0]),
            rows,
            (((0,), (0,)), ((), ())),
            preferred_element_type=jnp.float32,
        ).astype(jnp.bfloat16)

    asked[me] = requests[me]
    returned[me] = rows_of(requests[me])
    answers = []
    for j, source in enumerate(sources):
        asking[j].wait_recv()
        found[j] = rows_of(asked[source])
        copy = pltpu.make_async_remote_copy(
            found.at[j], returned.at[me], sems.at[2, j], sems.at[3, j], (source, rep), MESH
        )
        copy.start()
        answers.append(copy)
    asked_out[...] = asked[...]
    for j in range(n - 1):
        asking[j].wait_send()
        answers[j].wait()
    returned_out[...] = returned[...]


def fetch(requests, table):
    n, cap = requests.shape
    width = table.shape[1]
    vmem = pl.BlockSpec(memory_space=pltpu.VMEM)
    asked, returned = pl.pallas_call(
        functools.partial(fetch_kernel, n),
        out_shape=(
            jax.ShapeDtypeStruct((n, 1, cap), jnp.int32),
            jax.ShapeDtypeStruct((n, cap, width), jnp.bfloat16),
        ),
        in_specs=[vmem] * 2,
        out_specs=(vmem, vmem),
        scratch_shapes=[
            pltpu.VMEM((n, 1, cap), jnp.int32),
            pltpu.VMEM((n - 1, cap, width), jnp.bfloat16),
            pltpu.VMEM((n, cap, width), jnp.bfloat16),
            pltpu.SemaphoreType.DMA((4, n - 1)),
        ],
        compiler_params=pltpu.CompilerParams(collective_id=0, has_side_effects=True),
    )(requests.reshape(n, 1, cap), table)
    return asked, returned


def combine_kernel(
    n, links, top, hot, outgoing, asked, table, accum,
    top_out, hot_out, table_out, accum_out,
    incoming, cold, cold_half, cold_got, cold_last, table_all, accum_all,
    top_got, a_parts, a_gots, b_parts, b_gots, h_parts, h_gots, h_news, sends, recvs,
):
    me, rep = lax.axis_index("dp"), lax.axis_index("rep")
    core, side = bit_of(rep, 1), bit_of(rep, 2)
    over_core, over_side = (me, flipped(rep, 1)), (me, flipped(rep, 2))
    weights = [1 << k for k in range(links)]
    dp_bits = [bit_of(me, weight) for weight in weights]
    over_dp = [(flipped(me, weight), rep) for weight in weights]
    peers = [lax.rem(me + j, n) for j in range(1, n)]
    sources = [lax.rem(me + n - j, n) for j in range(1, n)]
    greet([(peer, rep) for peer in peers] + [over_core, over_side])
    count = [0]

    def send(src, dst, device):
        k = count[0]
        count[0] += 1
        copy = pltpu.make_async_remote_copy(src, dst, sends.at[k], recvs.at[k], device, MESH)
        copy.start()
        return copy

    hot_copy = send(hot.at[:, 1 - core], h_gots[0], over_core)
    top_copy = send(top.at[:, 1 - core], top_got, over_core)
    cold_copies = [
        send(outgoing.at[peer], incoming.at[me], (peer, rep)) for peer in peers
    ]

    a_route = [(side, over_side)] + list(zip(dp_bits, over_dp))
    b_route = [(dp_bits[0], over_dp[0]), (side, over_side)] + list(zip(dp_bits, over_dp))[1:]
    h_route = [(core, over_core)] + a_route

    def step_on(parts, gots, route, k, copy):
        bit = route[k][0]
        copy.wait()
        kept = parts[k][:, bit] + gots[k][...]
        if k + 1 == len(route):
            return kept
        parts[k + 1][...] = kept.reshape(parts[k + 1].shape)
        next_bit, device = route[k + 1]
        return send(parts[k + 1].at[:, 1 - next_bit], gots[k + 1], device)

    all_h = [hot] + list(h_parts)
    hot_state = [0, hot_copy]

    def spread(i):
        bit, device = h_route[len(h_route) - 1 - i]
        cur, new = h_news[2 * i], h_news[2 * i + 1]
        hot_state[1] = send(cur, new.at[:, bit], device)
        new[:, bit] = cur[...]

    def advance_hot():
        k, copy = hot_state
        i = k - len(h_route)
        hot_state[0] = k + 1
        if i >= 0:
            copy.wait()
            if i + 1 < len(h_route):
                cur = h_news[2 * i + 2]
                cur[...] = h_news[2 * i + 1][...].reshape(cur.shape)
                spread(i + 1)
        else:
            result = step_on(all_h, h_gots, h_route, k, copy)
            if i == -1:
                h_news[0][...] = result
                spread(0)
            else:
                hot_state[1] = result

    advance_hot()
    top_copy.wait()
    half = top.shape[3] // 2
    a_parts[0][...] = (top[:, core, :, :half] + top_got[:, :, :half]).reshape(a_parts[0].shape)
    a_copy = send(a_parts[0].at[:, 1 - side], a_gots[0], over_side)
    b_parts[0][...] = (top[:, core, :, half:] + top_got[:, :, half:]).reshape(b_parts[0].shape)
    b_copy = send(b_parts[0].at[:, 1 - dp_bits[0]], b_gots[0], over_dp[0])
    advance_hot()

    own_rows = table.shape[0] * table.shape[1]
    total = jnp.dot(
        chosen(asked[me], own_rows), outgoing[me], preferred_element_type=jnp.float32
    )
    for j, source in enumerate(sources):
        cold_copies[j].wait_recv()
        total += jnp.dot(
            chosen(asked[source], own_rows), incoming[source], preferred_element_type=jnp.float32
        )
    cold[...] = total.reshape(cold.shape)
    cold_copy = send(cold.at[:, 1 - core], cold_got, over_core)
    advance_hot()
    cold_copy.wait()
    cold_half[...] = cold[:, core] + cold_got[...]
    cold_copy = send(cold_half.at[1 - side], cold_last, over_side)
    advance_hot()
    a_copy = step_on(a_parts, a_gots, a_route, 0, a_copy)
    b_copy = step_on(b_parts, b_gots, b_route, 0, b_copy)
    advance_hot()
    cold_copy.wait()
    table_next, accum_next = adagrad(table[rep], accum[rep], cold_half[side] + cold_last[...])
    table_all[side, core] = table_next
    accum_all[side, core] = accum_next
    pair = [send(ref.at[side, core], ref.at[side, core], over_side) for ref in (table_all, accum_all)]
    advance_hot()
    last = len(a_route)
    for k in range(1, last):
        a_copy = step_on(a_parts, a_gots, a_route, k, a_copy)
        b_copy = step_on(b_parts, b_gots, b_route, k, b_copy)
        if k == 1:
            for copy in pair:
                copy.wait()
            pair = [send(ref.at[:, core], ref.at[:, core], over_core) for ref in (table_all, accum_all)]
        if hot_state[0] < 2 * len(h_route):
            advance_hot()
    top_out[:, :half] = a_copy.reshape(top_out.shape[0], half)
    top_out[:, half:] = b_copy.reshape(top_out.shape[0], half)
    for copy in pair:
        copy.wait()
    table_out[...] = table_all[...]
    accum_out[...] = accum_all[...]
    while hot_state[0] < 2 * len(h_route):
        advance_hot()
    hot_out[...] = h_news[-1][...]
    for copy in cold_copies:
        copy.wait_send()


def combine(top, hot, outgoing, asked, table, accum):
    n, cap, width = outgoing.shape
    devices = 4 * n
    links = n.bit_length() - 1
    rows, columns = top.shape[0] // devices, top.shape[1]
    hot_rows = hot.shape[0] // devices
    quarter = table.shape[0] // 4
    half = columns // 2
    f32 = lambda *shape: pltpu.VMEM(shape, jnp.float32)
    steps = [2**k for k in range(links, -1, -1)]
    a_parts = [f32(m, 2, rows, half) for m in steps]
    a_gots = [f32(m, rows, half) for m in steps]
    b_parts = [f32(n // 2, 2, 2, rows, half), f32(n // 2, 2, rows, half)] + a_parts[2:]
    b_gots = [f32(n // 2, 2, rows, half), f32(n // 2, rows, half)] + a_gots[2:]
    h_parts = [f32(m, 2, hot_rows, width) for m in steps]
    h_gots = [f32(m, hot_rows, width) for m in [2 * n] + steps]
    h_news = []
    for m in steps[::-1] + [2 * n]:
        h_news += [f32(m, hot_rows, width), f32(m, 2, hot_rows, width)]
    copies = 1 + (n - 1) + 2 * (links + 1) + 2 * (links + 2) + 2 + 4
    vmem = pl.BlockSpec(memory_space=pltpu.VMEM)
    out = lambda *shape: jax.ShapeDtypeStruct(shape, jnp.float32)
    square = (2, 2, quarter, width)
    return pl.pallas_call(
        functools.partial(combine_kernel, n, links),
        out_shape=(
            out(rows, columns), out(2 * n, 2, hot_rows, width), out(*square), out(*square)
        ),
        in_specs=[vmem] * 6,
        out_specs=(vmem,) * 4,
        scratch_shapes=[
            pltpu.VMEM((n, cap, width), jnp.bfloat16),
            f32(*square),
            f32(2, quarter, width),
            f32(2, quarter, width),
            f32(quarter, width),
            f32(*square),
            f32(*square),
            f32(2 * n, rows, columns),
            a_parts, a_gots, b_parts, b_gots, h_parts, h_gots, h_news,
            pltpu.SemaphoreType.DMA((copies,)),
            pltpu.SemaphoreType.DMA((copies,)),
        ],
        compiler_params=pltpu.CompilerParams(collective_id=1, has_side_effects=True),
    )(
        top.reshape(2 * n, 2, rows, columns),
        hot.reshape(2 * n, 2, hot_rows, width),
        outgoing, asked,
        table.reshape(4, quarter, width),
        accum.reshape(4, quarter, width),
    )


def suits(n, rep_n, top_rows):
    return rep_n == 4 and n >= 2 and n & (n - 1) == 0 and top_rows % (8 * n * rep_n) == 0


def local(
    hot_ids,
    cold_owner,
    cold_offset,
    labels,
    top_weight,
    out_weight,
    cold_table,
    cold_accum,
    hot_cache,
    hot_accum,
    pending,
    refresh_blocks,
    block_clock,
):
    width = hot_cache.shape[1]
    samples = hot_ids.shape[0]
    hot_feats = hot_ids.shape[1]
    lookups = cold_offset.shape[0]
    cold_feats = lookups // samples
    owners_count = lax.axis_size("dp")
    capacity = max(2, 2 * lookups // owners_count)
    owners = cold_owner[:, 0]
    matches = (owners[:, None] == jnp.arange(owners_count, dtype=jnp.int32)[None, :]).astype(
        jnp.int32
    )
    before = jnp.arange(lookups)[:, None] > jnp.arange(lookups)[None, :]
    earlier = jnp.dot(
        before.astype(jnp.bfloat16),
        matches.astype(jnp.bfloat16),
        preferred_element_type=jnp.float32,
    ).astype(jnp.int32)
    positions = jnp.sum(earlier * matches, axis=1)
    targets = owners * capacity + positions
    places = jnp.arange(owners_count * capacity, dtype=jnp.int32)
    placed = targets[:, None] == places[None, :]
    requests = jnp.sum(jnp.where(placed, cold_offset[:, None], 0), axis=0)
    placed = placed.astype(jnp.bfloat16)
    requests = requests.reshape(owners_count, capacity)
    direct = suits(owners_count, lax.axis_size("rep"), top_weight.shape[0])
    if direct:
        asked, returned = fetch(requests, cold_table)
    else:
        asked = lax.all_to_all(requests, "dp", split_axis=0, concat_axis=0, tiled=True)
        found = cold_table[asked].astype(jnp.bfloat16)
        returned = lax.all_to_all(found, "dp", split_axis=0, concat_axis=0, tiled=True)
    cold_rows = jnp.dot(
        placed,
        returned.reshape(owners_count * capacity, width),
        preferred_element_type=jnp.float32,
    ).astype(jnp.bfloat16)
    cold_rows = cold_rows.reshape(samples, cold_feats, width)
    hot_rows = hot_cache[hot_ids].astype(jnp.bfloat16)
    inputs = jnp.concatenate([hot_rows, cold_rows], axis=1).reshape(
        samples, (hot_feats + cold_feats) * width
    )
    preact = jnp.dot(inputs, top_weight, preferred_element_type=jnp.float32)
    hidden = jax.nn.silu(preact).astype(jnp.bfloat16)
    hidden_wide = hidden.astype(jnp.float32)
    logits = jnp.dot(hidden_wide, out_weight, precision=lax.Precision.HIGHEST)
    errors = jax.nn.sigmoid(logits) - labels.astype(jnp.float32)
    gates = jax.nn.sigmoid(preact)
    slope = gates * (1.0 + preact * (1.0 - gates))
    dhidden = (errors[:, None] * out_weight[None, :] * slope).astype(jnp.bfloat16)
    head_term = jnp.dot(errors, hidden_wide, precision=lax.Precision.HIGHEST)
    top_part = lax.dot_general(
        inputs, dhidden, (((0,), (0,)), ((), ())), preferred_element_type=jnp.float32
    )
    dinputs = lax.dot_general(
        dhidden, top_weight, (((1,), (1,)), ((), ())), preferred_element_type=jnp.float32
    ).astype(jnp.bfloat16)
    dinputs = dinputs.reshape(samples, hot_feats + cold_feats, width)
    cold_dx = dinputs[:, hot_feats:].reshape(lookups, width)
    outgoing = lax.dot_general(
        placed, cold_dx, (((0,), (0,)), ((), ())), preferred_element_type=jnp.float32
    ).astype(jnp.bfloat16)
    outgoing = outgoing.reshape(owners_count, capacity, width)
    own_rows = cold_table.shape[0]
    quarter = own_rows // lax.axis_size("rep")
    hot_count = hot_cache.shape[0]
    blocks_count = hot_count // BLOCK
    hot_dx = dinputs[:, :hot_feats].reshape(samples * hot_feats, width)
    hot_named = (
        jnp.arange(hot_count, dtype=jnp.int32)[:, None] == hot_ids.reshape(-1)[None, :]
    ).astype(jnp.bfloat16)
    hot_grad = jnp.dot(hot_named, hot_dx, preferred_element_type=jnp.float32)
    carried = (pending + hot_grad).reshape(blocks_count, BLOCK, width)
    picked = carried[refresh_blocks]
    divisors = 1.0 + block_clock.astype(jnp.float32)
    named = refresh_blocks[:, None] == jnp.arange(blocks_count, dtype=jnp.int32)[None, :]
    refreshed = jnp.any(named, axis=0)[:, None, None]
    cache_blocks = hot_cache.reshape(blocks_count, BLOCK, width)
    accum_blocks = hot_accum.reshape(blocks_count, BLOCK, width)
    if direct:
        picked_rows = refresh_blocks.shape[0] * BLOCK
        head_rows = head_term.shape[0] // width
        even = 8 * owners_count * lax.axis_size("rep")
        spare = -(picked_rows + head_rows) % even
        summands = jnp.concatenate(
            [
                picked.reshape(picked_rows, width),
                head_term.reshape(head_rows, width),
                jnp.zeros((spare, width), jnp.float32),
            ]
        )
        top_grad, sums, cold_table_new, cold_accum_new = combine(
            top_part, summands, outgoing, asked, cold_table, cold_accum
        )
        cold_table_new = cold_table_new.reshape(own_rows, width)
        cold_accum_new = cold_accum_new.reshape(own_rows, width)
        sums = sums.reshape(-1, width)
        picked_sum = sums[:picked_rows].reshape(picked.shape)
        out_grad = sums[picked_rows : picked_rows + head_rows].reshape(-1)
    else:
        incoming = lax.all_to_all(outgoing, "dp", split_axis=0, concat_axis=0, tiled=True)
        cold_grad = (
            jnp.zeros((own_rows, width), jnp.float32)
            .at[asked.reshape(-1)]
            .add(incoming.reshape(-1, width).astype(jnp.float32))
        )
        cold_share = lax.psum_scatter(cold_grad, "rep", scatter_dimension=0, tiled=True)
        offset_rows = lax.axis_index("rep") * quarter
        table_share = lax.dynamic_slice_in_dim(cold_table, offset_rows, quarter, 0)
        accum_share = lax.dynamic_slice_in_dim(cold_accum, offset_rows, quarter, 0)
        table_updated, accum_updated = adagrad(table_share, accum_share, cold_share)
        cold_table_new, cold_accum_new = (
            lax.all_gather(table_updated, "rep", axis=0, tiled=True),
            lax.all_gather(accum_updated, "rep", axis=0, tiled=True),
        )
        top_grad = lax.psum_scatter(top_part, ("dp", "rep"), scatter_dimension=0, tiled=True)
        picked_sum, out_grad = lax.psum((picked, head_term), ("dp", "rep"))
    block_sums = jnp.zeros((), jnp.float32)
    for k in range(refresh_blocks.shape[0]):
        block_sums = jnp.where(named[k][:, None, None], picked_sum[k][None], block_sums)
    flush = block_sums / divisors[:, None, None]
    cache_next, accum_next = adagrad(cache_blocks, accum_blocks, flush)
    hot_cache_new = jnp.where(refreshed, cache_next, cache_blocks).reshape(hot_count, width)
    hot_accum_new = jnp.where(refreshed, accum_next, accum_blocks).reshape(hot_count, width)
    pending_new = jnp.where(refreshed, 0.0, carried).reshape(hot_count, width)
    return (
        cold_table_new,
        cold_accum_new,
        hot_cache_new,
        hot_accum_new,
        pending_new,
        top_grad,
        out_grad,
    )


def solution(mesh):
    in_specs = (
        P(("dp", "rep"), None),
        P(("dp", "rep"), None),
        P(("dp", "rep")),
        P(("dp", "rep")),
        P(),
        P(),
        P("dp", None),
        P("dp", None),
        P(),
        P(),
        P(("dp", "rep"), None),
        P(),
        P(),
    )
    out_specs = (
        P("dp", None),
        P("dp", None),
        P(),
        P(),
        P(("dp", "rep"), None),
        P(("dp", "rep"), None),
        P(),
    )
    return jax.shard_map(local, mesh=mesh, in_specs=in_specs, out_specs=out_specs, check_vma=False)
```

profile of v0, /device:TPU:0, one launch (start us, length us, event | category | flops | bytes accessed | tf_op | source)
XLA Modules:
  0.0 77.5 jit_solution(2222635578375705994)
XLA Ops:
  0.7 1.1 %fusion.7 = s32[512]{0:T(512)S(1)} fusion(s32[512]{0:T(512)} %bitcast.122), kind=kOutput, calls=%fused_computation.14 | convolution fusion | flops 4484608 | bytes 4096 | tf_op jit(solution)/shard_map/dot_general | solution.py:319
  1.7 0.7 multiply_add_fusion.1
  2.4 1.6 %select_reduce_fusion = s32[1024]{0:T(1024)} fusion(s32[512]{0:T(512)} %param.15, s32[512]{0:T(512)S(1)} %bitcast.116), kind=kLoop, calls=%fused_computation.3 | loop fusion | flops 1571840 | bytes 8192 | tf_op jit(solution)/shard_map/reduce_sum | solution.py:328
  4.0 17.4 %shard_map.180 = (s32[8,1,128]{2,1,0:T(1,128)}, bf16[8,128,128]{2,1,0:T(8,128)(2,1)}) custom-call(s32[8,1,128]{2,1,0:T(1,128)} %bitcast.115, f32[512,128]{1,0:T(8,128)} %table.1), custom_call_target="tpu_custom_call" | custom-call | tf_op jit(solution)/shard_map/pallas_call | solution.py:88
  21.4 1.5 %fusion.5 = bf16[512,128]{1,0:T(8,128)(2,1)S(1)} fusion(bf16[1024,128]{1,0:T(8,128)(2,1)} %bitcast.124, s32[512]{0:T(512)S(1)} %bitcast.117), kind=kOutput, calls=%fused_computation.11 | convolution fusion | flops 134807552 | bytes 395264 | tf_op jit(solution)/shard_map/dot_general | solution.py:338
  22.9 0.7 compare_select_fusion
  23.9 1.1 %gather_fusion = bf16[512,128]{1,0:T(8,128)(2,1)S(1)} fusion(f32[1024,128]{1,0:T(8,128)S(1)} %copy-done.1, s32[1024]{0:T(1024)S(1)} %pad_clamp_fusion.1), kind=kCustom, calls=%fused_computation | custom fusion | bytes 264192 | tf_op jit(solution)/shard_map/gather | solution.py:344
  25.0 0.3 pad_maximum_fusion
  25.5 0.5 multiply_convert_fusion.1
  26.1 0.5 fusion.22
  26.7 2.1 %fusion.11.top = f32[16,2,16,1024]{3,2,1,0:T(8,128)} fusion(bf16[16,2,16,256]{3,2,1,0:T(8,128)(2,1)S(1)} %bitcast.107, f32[256,1024]{1,0:T(8,128)S(1)} %get-tuple-element.33, f32[1024]{0:T(1024)S(1)} %copy-done.8, f32[256]{0:T(256)S(1)} %divide_subtract_fusion), kind=kOutput, calls=%fused_computation.23 | convolution fusion | flops 271056896 | bytes 3412992 | tf_op jit(solution)/shard_map/dot_general | solution.py:357
  28.7 0.3 fusion.23
  29.1 0.6 convolution_convert_fusion
  30.3 0.5 fusion.3
  30.8 0.6 gather_fusion.1
  31.4 0.8 %maximum_maximum_fusion = f32[512,128]{1,0:T(8,128)} fusion(f32[8,128]{1,0:T(8,128)S(1)} %bitcast.114, f32[384,128]{1,0:T(8,128)S(1)} %bitcast.100, f32[512]{0:T(512)S(1)} %pad.2.clone), kind=kLoop, calls=%fused_computation.33 | loop fusion | flops 131072 | bytes 464896 | tf_op jit(solution)/shard_map/concatenate | solution.py:390
  32.3 1.5 %fusion.4 = bf16[1024,128]{1,0:T(8,128)(2,1)} fusion(bf16[512,128]{1,0:T(8,128)(2,1)S(1)} %bitcast.112, s32[512]{0:T(512)S(1)} %bitcast.118), kind=kOutput, calls=%fused_computation.9 | convolution fusion | flops 134873088 | bytes 395264 | tf_op jit(solution)/shard_map/dot_general | solution.py:365
  33.8 36.5 %shard_map.181 = (f32[16,1024]{1,0:T(8,128)}, f32[16,2,16,128]{3,2,1,0:T(8,128)}, f32[2,2,128,128]{3,2,1,0:T(8,128)}, f32[2,2,128,128]{3,2,1,0:T(8,128)}) custom-call(f32[16,2,16,1024]{3,2,1,0:T(8,128)} %fusion.11.top, f32[16,2,16,128]{3,2,1,0:T(8,128)} %bitcast.95, bf16[8,128,128]{2,1,0:T(8,128)(2,1)} %bitcast.104, s32[8,1,128]{2,1,0:T(1,128)} %get-tuple-element.14.asked, ...), custom_call_target="tpu_custom_call" | custom-call | tf_op jit(solution)/shard_map/pallas_call | solution.py:258
  70.4 1.0 %fusion.20 = (f32[4,2,16,128]{3,2,1,0:T(8,128)S(1)}, f32[4,2,16,128]{3,2,1,0:T(8,128)S(1)}, f32[4,2,16,128]{3,2,1,0:T(8,128)S(1)}) fusion(f32[16,2,16,128]{3,2,1,0:T(8,128)} %get-tuple-element.17), kind=kLoop, calls=%fused_computation.57 | loop fusion | bytes 393216 | tf_op jit(solution)/shard_map/slice | solution.py:425
  71.6 2.6 %fusion.16 = (f32[1024,128]{1,0:T(8,128)}, f32[1024,128]{1,0:T(8,128)}, f32[1024,128]{1,0:T(8,128)}) fusion(f32[1024,128]{1,0:T(8,128)S(1)} %copy-done.2, f32[1024]{0:T(1024)S(1)} %broadcast_bitcast_fusion, f32[128,128]{1,0:T(8,128)S(1)} %bitcast.109, f32[128,128]{1,0:T(8,128)S(1)} %bitcast.110, f32[128,128]{1,0:T(8,128)S(1)} %bitcast.108, ...), kind=kLoop, calls=%fused_computation.30 | loop fusion | flops 1703936 | bytes 3350528 | tf_op jit(solution)/shard_map/jit(_where)/select_n | solution.py:429
  74.2 1.3 %slice_bitcast_fusion = f32[1024]{0:T(1024)} fusion(f32[512,128]{1,0:T(8,128)} %bitcast.111), kind=kLoop, calls=%fused_computation.39 | loop fusion | bytes 8192 | tf_op jit(solution)/shard_map/reshape | solution.py:404
  75.4 0.7 copy.37
  76.1 0.7 copy.38
  76.8 0.6 copy.39
  (44 shorter events, 1.6 us)
Async XLA Ops:
  0.6 24.8 %copy-start = (bf16[512,1024]{1,0:T(8,128)(2,1)S(1)}, bf16[512,1024]{1,0:T(8,128)(2,1)}, u32[]{:S(2)}) copy-start(bf16[512,1024]{1,0:T(8,128)(2,1)} %param.17) | copy-start | bytes 3145732
  0.6 23.3 %copy-start.1 = (f32[1024,128]{1,0:T(8,128)S(1)}, f32[1024,128]{1,0:T(8,128)}, u32[]{:S(2)}) copy-start(f32[1024,128]{1,0:T(8,128)} %param.21) | copy-start | bytes 1572868
  25.5 0.7 copy-start.8
  25.5 1.2 %copy-start.9 = (s32[256]{0:T(256)S(1)}, s32[256]{0:T(256)}, u32[]{:S(2)}) copy-start(s32[256]{0:T(256)} %param.16) | copy-start | bytes 3076
  29.1 0.9 %copy-start.7 = (s32[256,2]{0,1:T(2,128)S(1)}, s32[256,2]{0,1:T(2,128)}, u32[]{:S(2)}) copy-start(s32[256,2]{0,1:T(2,128)} %param.13) | copy-start | bytes 6148
  29.1 1.2 %copy-start.3 = (f32[1024,128]{1,0:T(8,128)S(1)}, f32[1024,128]{1,0:T(8,128)}, u32[]{:S(2)}) copy-start(f32[1024,128]{1,0:T(8,128)} %param.23) | copy-start | bytes 1572868
  29.7 1.1 %copy-start.11 = (s32[3]{0:T(128)S(1)}, s32[3]{0:T(128)}, u32[]{:S(2)}) copy-start(s32[3]{0:T(128)} %param.24) | copy-start | bytes 40
  32.2 38.1 %copy-start.10 = (s32[8]{0:T(128)S(1)}, s32[8]{0:T(128)}, u32[]{:S(2)}) copy-start(s32[8]{0:T(128)} %param.25) | copy-start | bytes 100
  32.2 39.4 %copy-start.2 = (f32[1024,128]{1,0:T(8,128)S(1)}, f32[1024,128]{1,0:T(8,128)}, u32[]{:S(2)}) copy-start(f32[1024,128]{1,0:T(8,128)} %param.22) | copy-start | bytes 1572868
  70.3 5.1 %copy-start.5 = (f32[2,2,128,128]{3,2,1,0:T(8,128)S(1)}, f32[2,2,128,128]{3,2,1,0:T(8,128)}, u32[]{:S(2)}) copy-start(f32[2,2,128,128]{3,2,1,0:T(8,128)} %get-tuple-element.15) | copy-start | bytes 786436
  70.4 5.7 %copy-start.4 = (f32[2,2,128,128]{3,2,1,0:T(8,128)S(1)}, f32[2,2,128,128]{3,2,1,0:T(8,128)}, u32[]{:S(2)}) copy-start(f32[2,2,128,128]{3,2,1,0:T(8,128)} %get-tuple-element.16) | copy-start | bytes 786436
  71.6 5.2 %copy-start.6 = (f32[16,1024]{1,0:T(8,128)S(1)}, f32[16,1024]{1,0:T(8,128)}, u32[]{:S(2)}) copy-start(f32[16,1024]{1,0:T(8,128)} %get-tuple-element.50) | copy-start | bytes 196612
where the time goes:
time: 77.8 us; the launch traced here: 77.5 us
  Pallas kernels  54 us (69%)
  matrix products  8.51 us (11%)
  local copies, waits for them, and re-layouts  7.35 us (9%)
  other arithmetic  6.74 us (9%)
  between operations  0.91 us (1%)
    pallas_call x1, Pallas kernels, combine(): pl.pallas_call(functools.partial(combine_kernel, n, links), out_shape=(ou...  36.5 us
    pallas_call x1, Pallas kernels, fetch(): pl.pallas_call(functools.partial(fetch_kernel, n), out_shape=(jax.ShapeDt...  17.4 us
    select_n x1, other arithmetic, local(): jnp.where(refreshed, accum_next, accum_blocks).reshape(hot_count, width)  2.56 us
    unnamed x29, local copies, waits for them, and re-layouts  2.4 us
    dot_general x1, matrix products, local(): lax.dot_general(inputs, dhidden, (((0,), (0,)), ((), ())), preferred_elem...  2.07 us
    reduce_sum x1, other arithmetic, local(): requests = jnp.sum(jnp.where(placed, cold_offset[:, None], 0), axis=0)  1.56 us

commit v1 on v0

v1 whole, which is shorter than its diff:
```python
import functools

import jax
import jax.numpy as jnp
from jax import lax
from jax.experimental import pallas as pl
from jax.experimental.pallas import tpu as pltpu
from jax.sharding import PartitionSpec as P

BLOCK = 128
MESH = pl.DeviceIdType.MESH


step_size = 0.5
epsilon = 1e-08


def adagrad(table_rows, accum_rows, gradient):
    accum_next = accum_rows + gradient * gradient
    return (table_rows - step_size * gradient / (jnp.sqrt(accum_next) + epsilon), accum_next)


def row_to_col(row, first, step, count):
    per = 128 // step
    shape = (per, 128)
    wanted = lax.broadcasted_iota(jnp.int32, shape, 1) == step * lax.broadcasted_iota(
        jnp.int32, shape, 0
    ) + first
    pieces = []
    for i in range(count // per):
        part = jnp.broadcast_to(row[:, i * 128 : (i + 1) * 128], shape)
        pieces.append(jnp.sum(jnp.where(wanted, part, 0.0), axis=1, keepdims=True))
    return jnp.concatenate(pieces, axis=0)


def col_to_row(col):
    shape = (128, 128)
    same = lax.broadcasted_iota(jnp.int32, shape, 0) == lax.broadcasted_iota(jnp.int32, shape, 1)
    pieces = []
    for i in range(col.shape[0] // 128):
        part = jnp.broadcast_to(col[i * 128 : (i + 1) * 128], shape)
        pieces.append(jnp.sum(jnp.where(same, part, 0.0), axis=0, keepdims=True))
    return jnp.concatenate(pieces, axis=1)


def one_hot(ids, shape, dim):
    match = lax.broadcasted_iota(jnp.int32, shape, dim) == jnp.broadcast_to(ids, shape)
    return jnp.where(match, 1.0, 0.0).astype(jnp.bfloat16)


def matmul(a, b, contract=(1, 0)):
    return lax.dot_general(
        a, b, (((contract[0],), (contract[1],)), ((), ())), preferred_element_type=jnp.float32
    )


def step_kernel(
    n, piece,
    hot_ids, owner, offset, labels, out_weight, blocks, weight, table, cache, pending,
    top_out, sums_out, cold_out, carried_out,
    weight_v, table_v, cache_v, pending_v, tables, requests, asked, look, placed_t, hot_t, own_hot,
    pre, gate, hidden, inputs_t, inputs_got, dh, dh_got, outgoing, incoming,
    top_a, top_b, got_a, got_b, sum_a, sum_b, fin_a, fin_b,
    cold, cold_got, cold_half, cold_last, cold_full, hot_sum, hot_got, hot_z, hot_all,
    loads, sends, recvs,
):
    me, rep = lax.axis_index("dp"), lax.axis_index("rep")
    x, z = lax.rem(me, 2), lax.div(me, 2)
    core, y = lax.rem(rep, 2), lax.div(rep, 2)
    depth = n // 2
    f32, bf16 = jnp.float32, jnp.bfloat16

    def flip(value, on):
        return 1 - value if on else value

    def near(mask):
        return (z * 2 + flip(x, mask & 4), flip(y, mask & 2) * 2 + flip(core, mask & 1))

    def along(k):
        return (lax.rem(z + k, depth) * 2 + x, rep)

    sibling = near(1)
    peers = [lax.rem(me + j, n) for j in range(1, n)]
    sources = [lax.rem(me + n - j, n) for j in range(1, n)]
    greeted = [(peer, rep) for peer in peers] + [near(m) for m in (1, 2, 3, 5, 6, 7)]
    barrier = pltpu.get_barrier_semaphore()
    for device in greeted:
        pl.semaphore_signal(barrier, inc=1, device_id=device, device_id_type=MESH)
    local = []
    for i, (src, dst) in enumerate(
        [(table, table_v), (cache, cache_v), (weight, weight_v), (pending, pending_v)]
    ):
        local.append(pltpu.make_async_copy(src, dst, loads.at[i]))
        local[-1].start()

    count = [0]
    started = []

    def send(src, dst, device):
        k = count[0]
        count[0] += 1
        copy = pltpu.make_async_remote_copy(src, dst, sends.at[k], recvs.at[k], device, MESH)
        copy.start()
        started.append(copy)
        return copy

    local[0].wait()
    tables[me] = table_v[...].astype(bf16)
    pl.semaphore_wait(barrier, len(greeted))
    spread = [send(tables.at[me, core], tables.at[me, core], (peer, rep)) for peer in peers]

    samples = hot_ids.shape[1]
    hot_feats = hot_ids.shape[0]
    lookups = owner.shape[1]
    feats = lookups // samples
    own_rows, width = tables.shape[1] * tables.shape[2], tables.shape[3]
    cap = requests.shape[2]
    hot_rows = cache_v.shape[0]
    columns = weight_v.shape[1]
    chunk = dh.shape[2]
    chunks = columns // chunk
    hot_in = hot_feats * width

    owner_row, offset_row = owner[...].astype(f32), offset[...].astype(f32)
    owner_col = jnp.concatenate(
        [row_to_col(owner_row, k, feats, samples) for k in range(feats)], axis=0
    )
    offset_col = jnp.concatenate(
        [row_to_col(offset_row, k, feats, samples) for k in range(feats)], axis=0
    )
    lanes = lax.broadcasted_iota(jnp.int32, (lookups, 128), 1)
    matches = jnp.where(lanes == owner_col.astype(jnp.int32), 1.0, 0.0)
    square = (lookups, lookups)
    before = lax.broadcasted_iota(jnp.int32, square, 1) < lax.broadcasted_iota(
        jnp.int32, square, 0
    )
    earlier = matmul(jnp.where(before, 1.0, 0.0).astype(bf16), matches.astype(bf16))
    target = owner_col * cap + jnp.sum(earlier * matches, axis=1, keepdims=True)
    target_int = target.astype(jnp.int32)
    for o in range(n):
        slots = lax.broadcasted_iota(jnp.int32, (lookups, cap), 1) + o * cap
        asks = jnp.where(slots == target_int, offset_col, 0.0)
        requests[o] = jnp.sum(asks, axis=0, keepdims=True).astype(jnp.int32)
    asking = [send(requests.at[peer], asked.at[me], (peer, rep)) for peer in peers]
    asked[me] = requests[me]

    global_col = (owner_col * own_rows + offset_col).astype(jnp.int32)
    for o in range(n):
        look[o] = one_hot(global_col - o * own_rows, (lookups, own_rows), 1)

    hot_col = jnp.concatenate(
        [row_to_col(hot_ids[k : k + 1].astype(f32), 0, 1, samples) for k in range(hot_feats)], axis=0
    )
    local[1].wait()
    hot_found = matmul(
        one_hot(hot_col.astype(jnp.int32), (hot_feats * samples, hot_rows), 1),
        cache_v[...].astype(bf16),
    )
    hot_x = [hot_found[k * samples : (k + 1) * samples] for k in range(hot_feats)]
    local[2].wait()
    hot_wide = jnp.concatenate(hot_x, axis=1).astype(bf16)
    for h in range(chunks):
        at = slice(h * chunk, (h + 1) * chunk)
        pre[:, at] = matmul(hot_wide, weight_v[:hot_in, at])

    forwards = []
    for j, source in enumerate(sources):
        spread[j].wait_recv()
        forwards.append(send(tables.at[source, core], tables.at[source, core], sibling))

    placed_t[...] = one_hot(
        col_to_row(target).astype(jnp.int32), (n * cap, lookups), 0
    )
    hot_t[...] = one_hot(
        jnp.concatenate([hot_ids[k : k + 1] for k in range(hot_feats)], axis=1),
        (hot_rows, hot_feats * samples), 0,
    )

    def looked(o):
        return matmul(look[o], tables[o].reshape(own_rows, width))

    cold_found = looked(me)
    for j, source in enumerate(sources):
        forwards[j].wait_recv()
        cold_found += looked(source)
    cold_x = [cold_found[k * samples : (k + 1) * samples] for k in range(feats)]
    inputs_t[...] = (
        jnp.concatenate([part.T for part in hot_x + cold_x], axis=0)
        .astype(bf16)
        .reshape(inputs_t.shape)
    )
    inputs_copy = send(inputs_t.at[:, 1 - core], inputs_got, sibling)

    cold_wide = jnp.concatenate(cold_x, axis=1).astype(bf16)
    logits = jnp.zeros((samples, 1), f32)
    for h in range(chunks):
        at = slice(h * chunk, (h + 1) * chunk)
        preact = pre[:, at] + matmul(cold_wide, weight_v[hot_in:, at])
        gates = jax.nn.sigmoid(preact)
        shown = (preact * gates).astype(bf16)
        hidden[:, at] = shown
        logits += jnp.sum(shown.astype(f32) * out_weight[:, at], axis=1, keepdims=True)
        gate[:, at] = out_weight[:, at] * (gates * (1.0 + preact * (1.0 - gates)))
    errors = jax.nn.sigmoid(logits) - row_to_col(labels[...].astype(f32), 0, 1, samples)
    dh_copies = []
    for h in range(chunks):
        at = slice(h * chunk, (h + 1) * chunk)
        dh[h] = (errors * gate[:, at]).astype(bf16)
        dh_copies.append(send(dh.at[h], dh_got.at[h], sibling))

    dinputs = matmul(dh[0], weight_v[:, :chunk], (1, 1))
    for h in range(1, chunks):
        dinputs += matmul(dh[h], weight_v[:, h * chunk : (h + 1) * chunk], (1, 1))
    dinputs = dinputs.astype(bf16)
    cold_dx = jnp.concatenate(
        [dinputs[:, hot_in + k * width : hot_in + (k + 1) * width] for k in range(feats)], axis=0
    )
    outgoing[...] = matmul(placed_t[...], cold_dx).astype(bf16).reshape(outgoing.shape)
    cold_copies = [send(outgoing.at[peer], incoming.at[me], (peer, rep)) for peer in peers]
    incoming[me] = outgoing[me]

    def top_part(h):
        mine = inputs_t[:, core].reshape(-1, samples)
        both = matmul(mine, dh[h])
        dh_copies[h].wait_recv()
        return both + matmul(inputs_got[...].reshape(-1, samples), dh_got[h])

    quads = [(flip(x, m & 4) * 2 + flip(y, m & 2), near(m)) for m in (2, 4, 6)]
    my_quad = x * 2 + y
    zs = [(lax.rem(z + k, depth), along(k)) for k in range(1, depth)]
    inputs_copy.wait_recv()
    half = columns // 2
    for h in range(chunks // 2, chunks):
        at = slice(h * chunk - half, (h + 1) * chunk - half)
        top_b[:, :, :, at] = top_part(h).reshape(top_b.shape[:3] + (chunk,))
    b_copies = [send(top_b.at[to], got_b.at[i], device) for i, (to, device) in enumerate(zs)]
    for h in range(chunks // 2):
        at = slice(h * chunk, (h + 1) * chunk)
        top_a[:, :, :, at] = top_part(h).reshape(top_a.shape[:3] + (chunk,))
    a_copies = [
        send(top_a.at[:, to], got_a.at[i], device) for i, (to, device) in enumerate(quads)
    ]

    hot_dx = jnp.concatenate(
        [dinputs[:, k * width : (k + 1) * width] for k in range(hot_feats)], axis=0
    )
    local[3].wait()
    carried_out[...] = pending_v[...] + matmul(hot_t[...], hot_dx)
    total_rows = hot_sum.shape[0]
    picks = blocks.shape[0]
    for k in range(picks):
        wanted = jnp.full((BLOCK, width), blocks[k])
        picked = carried_out[:BLOCK, :]
        for b in range(1, hot_rows // BLOCK):
            picked = jnp.where(wanted == b, carried_out[b * BLOCK : (b + 1) * BLOCK, :], picked)
        hot_sum[k * BLOCK : (k + 1) * BLOCK, :] = picked
    base = picks * BLOCK
    hot_sum[base:, :] = jnp.zeros((total_rows - base, width), f32)
    for h in range(chunks):
        head = jnp.sum(
            errors * hidden[:, h * chunk : (h + 1) * chunk].astype(f32), axis=0, keepdims=True
        )
        for i in range(chunk // width):
            row = base + h * (chunk // width) + i
            hot_sum[row : row + 1, :] = head[:, i * width : (i + 1) * width]

    def piece_of(ref, q):
        return ref.at[pl.ds(pl.multiple_of(q * piece, 8), piece)]

    def spot(m):
        return flip(x, m & 4) * 4 + flip(y, m & 2) * 2 + flip(core, m & 1)

    h_copies = [
        send(piece_of(hot_sum, spot(m)), hot_got.at[m - 1], near(m)) for m in range(1, 8)
    ]

    for o in range(n - 1):
        asking[o].wait_recv()
    for o in range(n):
        own_hot[:, o * cap : (o + 1) * cap] = one_hot(asked[o], (own_rows, cap), 0)

    for copy in h_copies:
        copy.wait_recv()
    mine = piece_of(hot_sum, spot(0))[...]
    for m in range(7):
        mine += hot_got[m]
    hot_z[z] = mine
    hz_copies = [send(hot_z.at[z], hot_z.at[z], device) for _, device in zs]

    for copy in cold_copies:
        copy.wait_recv()
    cold[...] = matmul(own_hot[...], incoming[...].reshape(n * cap, width)).reshape(cold.shape)
    cold_copy = send(cold.at[1 - core], cold_got, sibling)

    for copy in b_copies:
        copy.wait_recv()
    part = top_b[z]
    for i in range(depth - 1):
        part += got_b[i]
    sum_b[...] = part
    b_copies = [send(sum_b.at[to], fin_b.at[i], device) for i, (to, device) in enumerate(quads)]

    cold_copy.wait_recv()
    cold_half[...] = cold[core] + cold_got[...]
    cold_copy = send(cold_half, cold_last, near(2))

    for copy in a_copies:
        copy.wait_recv()
    part = top_a[:, my_quad]
    for i in range(3):
        part += got_a[i]
    sum_a[...] = part
    a_copies = [send(sum_a.at[to], fin_a.at[i], device) for i, (to, device) in enumerate(zs)]

    for copy in hz_copies:
        copy.wait_recv()
    final = hot_z[0]
    for k in range(1, depth):
        final += hot_z[k]
    piece_of(hot_all, spot(0))[...] = final
    hot_copies = [
        send(piece_of(hot_all, spot(0)), piece_of(hot_all, spot(0)), near(m)) for m in range(1, 8)
    ]

    cold_copy.wait_recv()
    cold_full[core] = cold_half[...] + cold_last[...]
    cold_copy = send(cold_full.at[core], cold_full.at[core], sibling)

    for copy in b_copies:
        copy.wait_recv()
    part = sum_b[my_quad]
    for i in range(3):
        part += fin_b[i]
    top_out[:, half:] = part
    for copy in a_copies:
        copy.wait_recv()
    part = sum_a[z]
    for i in range(depth - 1):
        part += fin_a[i]
    top_out[:, :half] = part
    for copy in hot_copies:
        copy.wait_recv()
    sums_out[...] = hot_all[...]
    cold_copy.wait_recv()
    cold_out[...] = cold_full[...].reshape(cold_out.shape)
    for copy in started:
        copy.wait_send()


def step(hot_ids, owner, offset, labels, out_weight, blocks, weight, table, cache, pending, n, cap):
    hot_feats, samples = hot_ids.shape
    lookups = owner.shape[1]
    features, columns = weight.shape
    own_rows, width = table.shape
    hot_rows = cache.shape[0]
    depth = n // 2
    rows = features // (4 * n)
    half, chunk = columns // 2, columns // 4
    sum_rows = blocks.shape[0] * BLOCK + columns // width
    piece = -(-sum_rows // 64) * 8
    f32 = lambda *shape: pltpu.VMEM(shape, jnp.float32)
    b16 = lambda *shape: pltpu.VMEM(shape, jnp.bfloat16)
    i32 = lambda *shape: pltpu.VMEM(shape, jnp.int32)
    copies = 4 * (n - 1) + 1 + 4 + 2 * (depth - 1 + 3) + 7 + depth - 1 + 7 + 3
    vmem = pl.BlockSpec(memory_space=pltpu.VMEM)
    hbm = pl.BlockSpec(memory_space=pl.ANY)
    out = lambda *shape: jax.ShapeDtypeStruct(shape, jnp.float32)
    return pl.pallas_call(
        functools.partial(step_kernel, n, piece),
        out_shape=(
            out(rows, columns), out(8 * piece, width), out(own_rows, width), out(hot_rows, width)
        ),
        in_specs=[vmem] * 5 + [pl.BlockSpec(memory_space=pltpu.SMEM)] + [hbm] * 4,
        out_specs=(vmem,) * 4,
        scratch_shapes=[
            b16(features, columns), f32(2, own_rows // 2, width), f32(hot_rows, width),
            f32(hot_rows, width), b16(n, 2, own_rows // 2, width), i32(n, 1, cap), i32(n, 1, cap),
            b16(n, lookups, own_rows), b16(n * cap, lookups), b16(hot_rows, hot_feats * samples),
            b16(own_rows, n * cap),
            f32(samples, columns), f32(samples, columns), b16(samples, columns),
            b16(4 * depth, 2, rows, samples), b16(4 * depth, rows, samples),
            b16(4, samples, chunk), b16(4, samples, chunk),
            b16(n, cap, width), b16(n, cap, width),
            f32(depth, 4, rows, half), f32(depth, 4, rows, half),
            f32(3, depth, rows, half), f32(depth - 1, 4, rows, half),
            f32(depth, rows, half), f32(4, rows, half),
            f32(depth - 1, rows, half), f32(3, rows, half),
            f32(2, own_rows // 2, width), f32(own_rows // 2, width), f32(own_rows // 2, width),
            f32(own_rows // 2, width), f32(2, own_rows // 2, width),
            f32(8 * piece, width), f32(7, piece, width), f32(depth, piece, width),
            f32(8 * piece, width),
            pltpu.SemaphoreType.DMA((4,)),
            pltpu.SemaphoreType.DMA((copies,)),
            pltpu.SemaphoreType.DMA((copies,)),
        ],
        compiler_params=pltpu.CompilerParams(collective_id=0, has_side_effects=True),
    )(
        hot_ids, owner, offset, labels, out_weight, blocks,
        weight, table.reshape(2, own_rows // 2, width), cache, pending,
    )


def update_kernel(
    blocks, clock, top, sums, cold, carried, table, accum, cache, hot_accum,
    table_out, accum_out, cache_out, hot_accum_out, pending_out, top_out, head_out,
):
    table_out[...], accum_out[...] = adagrad(table[...], accum[...], cold[...])
    cache_out[...] = cache[...]
    hot_accum_out[...] = hot_accum[...]
    pending_out[...] = carried[...]
    picks = blocks.shape[0]
    for k in range(picks):
        rows = pl.ds(pl.multiple_of(blocks[k] * BLOCK, BLOCK), BLOCK)
        divisor = 1.0 + clock[blocks[k]].astype(jnp.float32)
        flush = sums[k * BLOCK : (k + 1) * BLOCK, :] / divisor
        cache_next, accum_next = adagrad(cache[rows, :], hot_accum[rows, :], flush)
        cache_out[rows, :] = cache_next
        hot_accum_out[rows, :] = accum_next
        pending_out[rows, :] = jnp.zeros((BLOCK, cache.shape[1]), jnp.float32)
    top_out[...] = top[...]
    head_out[...] = sums[picks * BLOCK : picks * BLOCK + head_out.shape[0], :]


def update(blocks, clock, top, sums, cold, carried, table, accum, cache, hot_accum):
    head_rows = top.shape[1] // cache.shape[1]
    smem = pl.BlockSpec(memory_space=pltpu.SMEM)
    vmem = pl.BlockSpec(memory_space=pltpu.VMEM)
    like = lambda a: jax.ShapeDtypeStruct(a.shape, a.dtype)
    return pl.pallas_call(
        update_kernel,
        out_shape=(
            like(table), like(accum), like(cache), like(hot_accum), like(carried), like(top),
            jax.ShapeDtypeStruct((head_rows, cache.shape[1]), jnp.float32),
        ),
        in_specs=[smem] * 2 + [vmem] * 8,
        out_specs=(vmem,) * 7,
    )(blocks, clock, top, sums, cold, carried, table, accum, cache, hot_accum)


def suits(n, rep_n, top_weight, hot_ids, cold_offset, hot_cache, cold_table):
    features, columns = top_weight.shape
    samples, lookups, width = hot_ids.shape[0], cold_offset.shape[0], hot_cache.shape[1]
    return (
        rep_n == 4
        and n % 2 == 0
        and 4 <= n <= 16
        and features % (16 * 4 * n) == 0
        and columns % 1024 == 0
        and samples % 128 == 0
        and lookups == 2 * samples
        and width == 128
        and (2 * lookups // n) % 128 == 0
        and hot_cache.shape[0] % 128 == 0
        and cold_table.shape[0] % 256 == 0
    )


def direct(
    n, hot_ids, cold_owner, cold_offset, labels, top_weight, out_weight, cold_table, cold_accum,
    hot_cache, hot_accum, pending, refresh_blocks, block_clock,
):
    cap = 2 * cold_offset.shape[0] // n
    top, sums, cold, carried = step(
        hot_ids.T, cold_owner.reshape(1, -1), cold_offset.reshape(1, -1), labels.reshape(1, -1),
        out_weight.reshape(1, -1), refresh_blocks, top_weight, cold_table, hot_cache, pending, n, cap,
    )
    results = update(
        refresh_blocks, block_clock, top, sums, cold, carried, cold_table, cold_accum, hot_cache,
        hot_accum,
    )
    return results[:6] + (results[6].reshape(-1),)


def local(
    hot_ids,
    cold_owner,
    cold_offset,
    labels,
    top_weight,
    out_weight,
    cold_table,
    cold_accum,
    hot_cache,
    hot_accum,
    pending,
    refresh_blocks,
    block_clock,
):
    n, rep_n = lax.axis_size("dp"), lax.axis_size("rep")
    if suits(n, rep_n, top_weight, hot_ids, cold_offset, hot_cache, cold_table):
        return direct(
            n, hot_ids, cold_owner, cold_offset, labels, top_weight, out_weight, cold_table,
            cold_accum, hot_cache, hot_accum, pending, refresh_blocks, block_clock,
        )
    width = hot_cache.shape[1]
    samples = hot_ids.shape[0]
    hot_feats = hot_ids.shape[1]
    lookups = cold_offset.shape[0]
    cold_feats = lookups // samples
    owners_count = lax.axis_size("dp")
    capacity = max(2, 2 * lookups // owners_count)
    owners = cold_owner[:, 0]
    matches = (owners[:, None] == jnp.arange(owners_count, dtype=jnp.int32)[None, :]).astype(
        jnp.int32
    )
    before = jnp.arange(lookups)[:, None] > jnp.arange(lookups)[None, :]
    earlier = jnp.dot(
        before.astype(jnp.bfloat16),
        matches.astype(jnp.bfloat16),
        preferred_element_type=jnp.float32,
    ).astype(jnp.int32)
    positions = jnp.sum(earlier * matches, axis=1)
    targets = owners * capacity + positions
    places = jnp.arange(owners_count * capacity, dtype=jnp.int32)
    placed = targets[:, None] == places[None, :]
    requests = jnp.sum(jnp.where(placed, cold_offset[:, None], 0), axis=0)
    placed = placed.astype(jnp.bfloat16)
    requests = requests.reshape(owners_count, capacity)
    asked = lax.all_to_all(requests, "dp", split_axis=0, concat_axis=0, tiled=True)
    found = cold_table[asked].astype(jnp.bfloat16)
    returned = lax.all_to_all(found, "dp", split_axis=0, concat_axis=0, tiled=True)
    cold_rows = jnp.dot(
        placed,
        returned.reshape(owners_count * capacity, width),
        preferred_element_type=jnp.float32,
    ).astype(jnp.bfloat16)
    cold_rows = cold_rows.reshape(samples, cold_feats, width)
    hot_rows = hot_cache[hot_ids].astype(jnp.bfloat16)
    inputs = jnp.concatenate([hot_rows, cold_rows], axis=1).reshape(
        samples, (hot_feats + cold_feats) * width
    )
    preact = jnp.dot(inputs, top_weight, preferred_element_type=jnp.float32)
    hidden = jax.nn.silu(preact).astype(jnp.bfloat16)
    hidden_wide = hidden.astype(jnp.float32)
    logits = jnp.dot(hidden_wide, out_weight, precision=lax.Precision.HIGHEST)
    errors = jax.nn.sigmoid(logits) - labels.astype(jnp.float32)
    gates = jax.nn.sigmoid(preact)
    slope = gates * (1.0 + preact * (1.0 - gates))
    dhidden = (errors[:, None] * out_weight[None, :] * slope).astype(jnp.bfloat16)
    head_term = jnp.dot(errors, hidden_wide, precision=lax.Precision.HIGHEST)
    top_part = lax.dot_general(
        inputs, dhidden, (((0,), (0,)), ((), ())), preferred_element_type=jnp.float32
    )
    dinputs = lax.dot_general(
        dhidden, top_weight, (((1,), (1,)), ((), ())), preferred_element_type=jnp.float32
    ).astype(jnp.bfloat16)
    dinputs = dinputs.reshape(samples, hot_feats + cold_feats, width)
    cold_dx = dinputs[:, hot_feats:].reshape(lookups, width)
    outgoing = lax.dot_general(
        placed, cold_dx, (((0,), (0,)), ((), ())), preferred_element_type=jnp.float32
    ).astype(jnp.bfloat16)
    outgoing = outgoing.reshape(owners_count, capacity, width)
    own_rows = cold_table.shape[0]
    quarter = own_rows // lax.axis_size("rep")
    hot_count = hot_cache.shape[0]
    blocks_count = hot_count // BLOCK
    hot_dx = dinputs[:, :hot_feats].reshape(samples * hot_feats, width)
    hot_named = (
        jnp.arange(hot_count, dtype=jnp.int32)[:, None] == hot_ids.reshape(-1)[None, :]
    ).astype(jnp.bfloat16)
    hot_grad = jnp.dot(hot_named, hot_dx, preferred_element_type=jnp.float32)
    carried = (pending + hot_grad).reshape(blocks_count, BLOCK, width)
    picked = carried[refresh_blocks]
    divisors = 1.0 + block_clock.astype(jnp.float32)
    named = refresh_blocks[:, None] == jnp.arange(blocks_count, dtype=jnp.int32)[None, :]
    refreshed = jnp.any(named, axis=0)[:, None, None]
    cache_blocks = hot_cache.reshape(blocks_count, BLOCK, width)
    accum_blocks = hot_accum.reshape(blocks_count, BLOCK, width)
    incoming = lax.all_to_all(outgoing, "dp", split_axis=0, concat_axis=0, tiled=True)
    cold_grad = (
        jnp.zeros((own_rows, width), jnp.float32)
        .at[asked.reshape(-1)]
        .add(incoming.reshape(-1, width).astype(jnp.float32))
    )
    cold_share = lax.psum_scatter(cold_grad, "rep", scatter_dimension=0, tiled=True)
    offset_rows = lax.axis_index("rep") * quarter
    table_share = lax.dynamic_slice_in_dim(cold_table, offset_rows, quarter, 0)
    accum_share = lax.dynamic_slice_in_dim(cold_accum, offset_rows, quarter, 0)
    table_updated, accum_updated = adagrad(table_share, accum_share, cold_share)
    cold_table_new, cold_accum_new = (
        lax.all_gather(table_updated, "rep", axis=0, tiled=True),
        lax.all_gather(accum_updated, "rep", axis=0, tiled=True),
    )
    top_grad = lax.psum_scatter(top_part, ("dp", "rep"), scatter_dimension=0, tiled=True)
    picked_sum, out_grad = lax.psum((picked, head_term), ("dp", "rep"))
    block_sums = jnp.zeros((), jnp.float32)
    for k in range(refresh_blocks.shape[0]):
        block_sums = jnp.where(named[k][:, None, None], picked_sum[k][None], block_sums)
    flush = block_sums / divisors[:, None, None]
    cache_next, accum_next = adagrad(cache_blocks, accum_blocks, flush)
    hot_cache_new = jnp.where(refreshed, cache_next, cache_blocks).reshape(hot_count, width)
    hot_accum_new = jnp.where(refreshed, accum_next, accum_blocks).reshape(hot_count, width)
    pending_new = jnp.where(refreshed, 0.0, carried).reshape(hot_count, width)
    return (
        cold_table_new,
        cold_accum_new,
        hot_cache_new,
        hot_accum_new,
        pending_new,
        top_grad,
        out_grad,
    )


def solution(mesh):
    in_specs = (
        P(("dp", "rep"), None),
        P(("dp", "rep"), None),
        P(("dp", "rep")),
        P(("dp", "rep")),
        P(),
        P(),
        P("dp", None),
        P("dp", None),
        P(),
        P(),
        P(("dp", "rep"), None),
        P(),
        P(),
    )
    out_specs = (
        P("dp", None),
        P("dp", None),
        P(),
        P(),
        P(("dp", "rep"), None),
        P(("dp", "rep"), None),
        P(),
    )
    return jax.shard_map(local, mesh=mesh, in_specs=in_specs, out_specs=out_specs, check_vma=False)
```

time: 77.8 us -> 56.2 us (0.72)
  matrix products: 8.51 us -> 0 us
  local copies, waits for them, and re-layouts: 7.35 us -> 0 us
  other arithmetic: 6.74 us -> 0 us
  Pallas kernels: 54 us -> 55.1 us
    dot_general x9 -> x0, matrix products: 8.51 us -> none  [the longest x1 2.07 us: local(): lax.dot_general(inputs, dhidden, (((0,), (0,)), ((), ())), preferred_elem...]
    select_n x3 -> x0, other arithmetic: 3.25 us -> none  [the longest x1 2.56 us: local(): jnp.where(refreshed, accum_next, accum_blocks).reshape(hot_count, width)]
    unnamed x29 -> x0, local copies, waits for them, and re-layouts: 2.4 us -> none
    gather x2 -> x0, local copies, waits for them, and re-layouts: 1.62 us -> none  [the longest x1 1.06 us: local(): hot_rows = hot_cache[hot_ids].astype(jnp.bfloat16)]
    reduce_sum x1 -> x0, other arithmetic: 1.56 us -> none  [local(): requests = jnp.sum(jnp.where(placed, cold_offset[:, None], 0), axis=0)]
    reshape x3 -> x0, local copies, waits for them, and re-layouts: 1.46 us -> none  [the longest x1 1.26 us: local(): out_grad = sums[picked_rows:picked_rows + head_rows].reshape(-1)]
    slice x2 -> x0, local copies, waits for them, and re-layouts: 1.14 us -> none  [the longest x1 0.96 us: local(): picked_sum[k][None]]
    pallas_call x2, Pallas kernels: 54 us -> 55.1 us  [the longest x1 51.8 us: step(): pl.pallas_call(functools.partial(step_kernel, n, piece), out_shape=(out(r...]
where the time goes in v1:
time: 56.2 us; the launch traced here: 55.7 us
  Pallas kernels  55.1 us (98%)
  between operations  0.64 us (1%)
    pallas_call x1, Pallas kernels, step(): pl.pallas_call(functools.partial(step_kernel, n, piece), out_shape=(out(r...  51.8 us
    pallas_call x1, Pallas kernels, update(): pl.pallas_call(update_kernel, out_shape=(like(table), like(accum), like(c...  3.3 us

profile of v1, /device:TPU:0, one launch (start us, length us, event | category | flops | bytes accessed | tf_op | source)
XLA Modules:
  0.0 55.7 jit_solution(18332730260521864924)
XLA Ops:
  0.6 51.8 %shard_map.180 = (f32[16,1024]{1,0:T(8,128)}, f32[448,128]{1,0:T(8,128)}, f32[512,128]{1,0:T(8,128)}, f32[1024,128]{1,0:T(8,128)}) custom-call(s32[2,256]{1,0:T(2,128)} %bitcast.9, s32[1,512]{1,0:T(1,128)} %bitcast.10, s32[1,512]{1,0:T(1,128)} %bitcast.11, s32[1,256]{1,0:T(1,128)} %bitcast.12, f32[1,1024]{1,0:T(1,128)} %bitcast.8, s32[3]{0:T(128)} %blocks.3, ...), custom_call_target="tpu_custom_call" | custom-call | tf_op jit(solution)/shard_map/pallas_call | solution.py:368
  52.4 3.3 %shard_map.181 = (f32[512,128]{1,0:T(8,128)}, f32[512,128]{1,0:T(8,128)}, f32[1024,128]{1,0:T(8,128)}, f32[1024,128]{1,0:T(8,128)}, f32[1024,128]{1,0:T(8,128)}, /*index=5*/f32[16,1024]{1,0:T(8,128)}, f32[8,128]{1,0:T(8,128)}) custom-call(s32[3]{0:T(128)} %blocks.3, s32[8]{0:T(128)} %clock.1, f32[16,1024]{1,0:T(8,128)} %get-tuple-element.18.top, ...), custom_call_target="tpu_custom_call" | custom-call | tf_op jit(solution)/shard_map/pallas_call | solution.py:429

commit v2 on v1

--- a/solution.py
+++ b/solution.py
@@ -8,6 +8,7 @@
 from jax.sharding import PartitionSpec as P
 
 BLOCK = 128
+VMEM_LIMIT = 40 * 1024 * 1024
 MESH = pl.DeviceIdType.MESH
 
 
@@ -56,12 +57,15 @@
 
 def step_kernel(
     n, piece,
-    hot_ids, owner, offset, labels, out_weight, blocks, weight, table, cache, pending,
+    hot_ids_in, owner_in, offset_in, labels_in, out_weight_in, blocks_in, weight, table, cache,
+    pending,
     top_out, sums_out, cold_out, carried_out,
-    weight_v, table_v, cache_v, pending_v, tables, requests, asked, look, placed_t, hot_t, own_hot,
+    hot_ids, owner, offset, labels, out_weight, blocks,
+    weight_v, table_v, table_all, cache_v, pending_v, tables, requests, asked, look, placed_t, hot_t, own_hot,
     pre, gate, hidden, inputs_t, inputs_got, dh, dh_got, outgoing, incoming,
-    top_a, top_b, got_a, got_b, sum_a, sum_b, fin_a, fin_b,
-    cold, cold_got, cold_half, cold_last, cold_full, hot_sum, hot_got, hot_z, hot_all,
+    top, leave, got_1, part_1, got_2, part_2, got_3,
+    cold, cold_got, cold_half, cold_last, cold_full, hot_sum, hot_got, hot_mid, hot_near, hot_z,
+    hot_all,
     loads, sends, recvs,
 ):
     me, rep = lax.axis_index("dp"), lax.axis_index("rep")
@@ -77,20 +81,23 @@
         return (z * 2 + flip(x, mask & 4), flip(y, mask & 2) * 2 + flip(core, mask & 1))
 
     def along(k):
-        return (lax.rem(z + k, depth) * 2 + x, rep)
-
-    sibling = near(1)
+        return lax.rem(z + k, depth) * 2 + x
+
+    sibling, over_x, over_y = near(1), near(4), near(2)
     peers = [lax.rem(me + j, n) for j in range(1, n)]
     sources = [lax.rem(me + n - j, n) for j in range(1, n)]
-    greeted = [(peer, rep) for peer in peers] + [near(m) for m in (1, 2, 3, 5, 6, 7)]
+    greeted = [(peer, rep) for peer in peers] + [sibling, over_y, near(6)]
     barrier = pltpu.get_barrier_semaphore()
     for device in greeted:
         pl.semaphore_signal(barrier, inc=1, device_id=device, device_id_type=MESH)
     local = []
-    for i, (src, dst) in enumerate(
-        [(table, table_v), (cache, cache_v), (weight, weight_v), (pending, pending_v)]
-    ):
-        local.append(pltpu.make_async_copy(src, dst, loads.at[i]))
+    for src, dst in [
+        (table.at[rep], table_v.at[rep]), (owner_in, owner), (offset_in, offset),
+        (table, table_all), (hot_ids_in, hot_ids), (cache, cache_v),
+        (weight, weight_v), (labels_in, labels), (out_weight_in, out_weight), (blocks_in, blocks),
+        (pending, pending_v),
+    ]:
+        local.append(pltpu.make_async_copy(src, dst, loads.at[len(local)]))
         local[-1].start()
 
     count = [0]
@@ -104,10 +111,16 @@
         started.append(copy)
         return copy
 
+    def same(ref, device):
+        return send(ref, ref, device)
+
     local[0].wait()
-    tables[me] = table_v[...].astype(bf16)
+    tables[me, rep] = table_v[rep].astype(bf16)
     pl.semaphore_wait(barrier, len(greeted))
-    spread = [send(tables.at[me, core], tables.at[me, core], (peer, rep)) for peer in peers]
+    mine = tables.at[me, rep]
+    order = sorted(range(1, depth), key=lambda k: abs(2 * k - depth))
+    z_table = {k: same(mine, (along(k), rep)) for k in order}
+    x_table = same(mine, over_x)
 
     samples = hot_ids.shape[1]
     hot_feats = hot_ids.shape[0]
@@ -121,6 +134,8 @@
     chunks = columns // chunk
     hot_in = hot_feats * width
 
+    local[1].wait()
+    local[2].wait()
     owner_row, offset_row = owner[...].astype(f32), offset[...].astype(f32)
     owner_col = jnp.concatenate(
         [row_to_col(owner_row, k, feats, samples) for k in range(feats)], axis=0
@@ -148,26 +163,55 @@
     for o in range(n):
         look[o] = one_hot(global_col - o * own_rows, (lookups, own_rows), 1)
 
+    def relay(copy, source, *devices):
+        copy.wait_recv()
+        return [same(tables.at[source, rep], device) for device in devices]
+
+    def looked(o):
+        return matmul(look[o], tables[o].reshape(own_rows, width))
+
+    order = order[::-1]
+    x_source = z * 2 + 1 - x
+    z_source = {k: lax.rem(z + depth - k, depth) * 2 + x for k in order}
+    far_source = {k: lax.rem(z + depth - k, depth) * 2 + 1 - x for k in order}
+    others = [x_source] + [z_source[k] for k in order] + [far_source[k] for k in order]
+    by_y, by_core, y_core, by_x = {}, {}, {}, {}
+    by_y[0], by_core[0] = relay(x_table, x_source, over_y, sibling)
+
+    local[4].wait()
     hot_col = jnp.concatenate(
         [row_to_col(hot_ids[k : k + 1].astype(f32), 0, 1, samples) for k in range(hot_feats)], axis=0
     )
-    local[1].wait()
+    local[5].wait()
     hot_found = matmul(
         one_hot(hot_col.astype(jnp.int32), (hot_feats * samples, hot_rows), 1),
         cache_v[...].astype(bf16),
     )
     hot_x = [hot_found[k * samples : (k + 1) * samples] for k in range(hot_feats)]
-    local[2].wait()
+
+    for i, k in enumerate(order):
+        by_x[k], by_y[1 + i], by_core[1 + i] = relay(
+            z_table[k], z_source[k], over_x, over_y, sibling
+        )
+
+    local[6].wait()
     hot_wide = jnp.concatenate(hot_x, axis=1).astype(bf16)
     for h in range(chunks):
         at = slice(h * chunk, (h + 1) * chunk)
         pre[:, at] = matmul(hot_wide, weight_v[:hot_in, at])
-
-    forwards = []
-    for j, source in enumerate(sources):
-        spread[j].wait_recv()
-        forwards.append(send(tables.at[source, core], tables.at[source, core], sibling))
-
+    local[3].wait()
+    for i in range(1, 4):
+        tables[me, lax.rem(rep + i, 4)] = table_all[lax.rem(rep + i, 4)].astype(bf16)
+
+    def relay_y(i):
+        by_y[i].wait_recv()
+        y_core[i] = same(tables.at[others[i], (1 - y) * 2 + core], sibling)
+
+    relay_y(0)
+    cold_found = looked(me)
+    for i, k in enumerate(order):
+        by_y[depth + i], by_core[depth + i] = relay(by_x[k], far_source[k], over_y, sibling)
+        relay_y(1 + i)
     placed_t[...] = one_hot(
         col_to_row(target).astype(jnp.int32), (n * cap, lookups), 0
     )
@@ -175,14 +219,16 @@
         jnp.concatenate([hot_ids[k : k + 1] for k in range(hot_feats)], axis=1),
         (hot_rows, hot_feats * samples), 0,
     )
-
-    def looked(o):
-        return matmul(look[o], tables[o].reshape(own_rows, width))
-
-    cold_found = looked(me)
-    for j, source in enumerate(sources):
-        forwards[j].wait_recv()
-        cold_found += looked(source)
+    for i in range(depth, n - 1):
+        relay_y(i)
+        j = i - depth
+        by_core[j].wait_recv()
+        y_core[j].wait_recv()
+        cold_found += looked(others[j])
+    for j in range(depth - 1, n - 1):
+        by_core[j].wait_recv()
+        y_core[j].wait_recv()
+        cold_found += looked(others[j])
     cold_x = [cold_found[k * samples : (k + 1) * samples] for k in range(feats)]
     inputs_t[...] = (
         jnp.concatenate([part.T for part in hot_x + cold_x], axis=0)
@@ -191,6 +237,8 @@
     )
     inputs_copy = send(inputs_t.at[:, 1 - core], inputs_got, sibling)
 
+    local[7].wait()
+    local[8].wait()
     cold_wide = jnp.concatenate(cold_x, axis=1).astype(bf16)
     logits = jnp.zeros((samples, 1), f32)
     for h in range(chunks):
@@ -219,32 +267,11 @@
     cold_copies = [send(outgoing.at[peer], incoming.at[me], (peer, rep)) for peer in peers]
     incoming[me] = outgoing[me]
 
-    def top_part(h):
-        mine = inputs_t[:, core].reshape(-1, samples)
-        both = matmul(mine, dh[h])
-        dh_copies[h].wait_recv()
-        return both + matmul(inputs_got[...].reshape(-1, samples), dh_got[h])
-
-    quads = [(flip(x, m & 4) * 2 + flip(y, m & 2), near(m)) for m in (2, 4, 6)]
-    my_quad = x * 2 + y
-    zs = [(lax.rem(z + k, depth), along(k)) for k in range(1, depth)]
-    inputs_copy.wait_recv()
-    half = columns // 2
-    for h in range(chunks // 2, chunks):
-        at = slice(h * chunk - half, (h + 1) * chunk - half)
-        top_b[:, :, :, at] = top_part(h).reshape(top_b.shape[:3] + (chunk,))
-    b_copies = [send(top_b.at[to], got_b.at[i], device) for i, (to, device) in enumerate(zs)]
-    for h in range(chunks // 2):
-        at = slice(h * chunk, (h + 1) * chunk)
-        top_a[:, :, :, at] = top_part(h).reshape(top_a.shape[:3] + (chunk,))
-    a_copies = [
-        send(top_a.at[:, to], got_a.at[i], device) for i, (to, device) in enumerate(quads)
-    ]
-
     hot_dx = jnp.concatenate(
         [dinputs[:, k * width : (k + 1) * width] for k in range(hot_feats)], axis=0
     )
-    local[3].wait()
+    local[9].wait()
+    local[10].wait()
     carried_out[...] = pending_v[...] + matmul(hot_t[...], hot_dx)
     total_rows = hot_sum.shape[0]
     picks = blocks.shape[0]
@@ -264,85 +291,100 @@
             row = base + h * (chunk // width) + i
             hot_sum[row : row + 1, :] = head[:, i * width : (i + 1) * width]
 
-    def piece_of(ref, q):
-        return ref.at[pl.ds(pl.multiple_of(q * piece, 8), piece)]
-
-    def spot(m):
-        return flip(x, m & 4) * 4 + flip(y, m & 2) * 2 + flip(core, m & 1)
-
-    h_copies = [
-        send(piece_of(hot_sum, spot(m)), hot_got.at[m - 1], near(m)) for m in range(1, 8)
-    ]
+    def part_of(ref, q, rows):
+        return ref.at[pl.ds(pl.multiple_of(q * rows, 8), rows)]
+
+    hot_copy = send(part_of(hot_sum, 1 - core, 4 * piece), hot_got, sibling)
+    my_quad = x * 2 + y
+    quads = [(flip(x, m & 4) * 2 + flip(y, m & 2), near(m)) for m in (2, 4, 6)]
+
+    inputs_copy.wait_recv()
+
+    def first_step(h):
+        both = matmul(inputs_t[:, core].reshape(-1, samples), dh[h])
+        dh_copies[h].wait_recv()
+        both += matmul(inputs_got[...].reshape(-1, samples), dh_got[h])
+        top[h] = both.reshape(top.shape[1:])
+        leaving = top[h, :, 1 - x] if h % 2 == 0 else top[h, :, :, 1 - y]
+        leave[h] = leaving.astype(bf16)
+        return send(leave.at[h], got_1.at[h], over_x if h % 2 == 0 else over_y)
+
+    def second_step(h):
+        first[h].wait_recv()
+        kept = top[h, :, x] if h % 2 == 0 else top[h, :, :, y]
+        part_1[h] = kept + got_1[h].astype(f32)
+        if h % 2 == 0:
+            return send(part_1.at[h, :, 1 - y], got_2.at[h], over_y)
+        return send(part_1.at[h, :, 1 - x], got_2.at[h], over_x)
+
+    def third_step(h):
+        second[h].wait_recv()
+        part_2[h] = part_1[h, :, y if h % 2 == 0 else x] + got_2[h]
+        return [
+            send(part_2.at[h, lax.rem(z + k, depth)], got_3.at[h, k - 1], (along(k), rep))
+            for k in range(1, depth)
+        ]
+
+    first = [first_step(h) for h in range(chunks)]
 
     for o in range(n - 1):
         asking[o].wait_recv()
     for o in range(n):
         own_hot[:, o * cap : (o + 1) * cap] = one_hot(asked[o], (own_rows, cap), 0)
 
-    for copy in h_copies:
+    hot_copy.wait_recv()
+    hot_mid[...] = part_of(hot_sum, core, 4 * piece)[...] + hot_got[...]
+    hot_copies = [
+        send(part_of(hot_mid, q, piece), hot_near.at[i], device)
+        for i, (q, device) in enumerate(quads)
+    ]
+
+    second = [second_step(h) for h in range(chunks)]
+
+    for copy in hot_copies:
         copy.wait_recv()
-    mine = piece_of(hot_sum, spot(0))[...]
-    for m in range(7):
-        mine += hot_got[m]
-    hot_z[z] = mine
-    hz_copies = [send(hot_z.at[z], hot_z.at[z], device) for _, device in zs]
+    hot_z[z] = part_of(hot_mid, my_quad, piece)[...] + hot_near[0] + hot_near[1] + hot_near[2]
+    hot_copies = [same(hot_z.at[z], (along(k), rep)) for k in range(1, depth)]
 
     for copy in cold_copies:
         copy.wait_recv()
     cold[...] = matmul(own_hot[...], incoming[...].reshape(n * cap, width)).reshape(cold.shape)
     cold_copy = send(cold.at[1 - core], cold_got, sibling)
 
-    for copy in b_copies:
-        copy.wait_recv()
-    part = top_b[z]
-    for i in range(depth - 1):
-        part += got_b[i]
-    sum_b[...] = part
-    b_copies = [send(sum_b.at[to], fin_b.at[i], device) for i, (to, device) in enumerate(quads)]
+    third = [third_step(h) for h in range(chunks)]
 
     cold_copy.wait_recv()
     cold_half[...] = cold[core] + cold_got[...]
-    cold_copy = send(cold_half, cold_last, near(2))
-
-    for copy in a_copies:
-        copy.wait_recv()
-    part = top_a[:, my_quad]
-    for i in range(3):
-        part += got_a[i]
-    sum_a[...] = part
-    a_copies = [send(sum_a.at[to], fin_a.at[i], device) for i, (to, device) in enumerate(zs)]
-
-    for copy in hz_copies:
+    cold_copy = send(cold_half, cold_last, over_y)
+
+    for copy in hot_copies:
         copy.wait_recv()
     final = hot_z[0]
     for k in range(1, depth):
         final += hot_z[k]
-    piece_of(hot_all, spot(0))[...] = final
-    hot_copies = [
-        send(piece_of(hot_all, spot(0)), piece_of(hot_all, spot(0)), near(m)) for m in range(1, 8)
-    ]
+    ours = core * 4 + my_quad
+    part_of(hot_all, ours, piece)[...] = final
+    hot_copies = [same(part_of(hot_all, ours, piece), device) for _, device in quads]
 
     cold_copy.wait_recv()
     cold_full[core] = cold_half[...] + cold_last[...]
-    cold_copy = send(cold_full.at[core], cold_full.at[core], sibling)
-
-    for copy in b_copies:
-        copy.wait_recv()
-    part = sum_b[my_quad]
-    for i in range(3):
-        part += fin_b[i]
-    top_out[:, half:] = part
-    for copy in a_copies:
-        copy.wait_recv()
-    part = sum_a[z]
-    for i in range(depth - 1):
-        part += fin_a[i]
-    top_out[:, :half] = part
+    cold_copy = same(cold_full.at[core], sibling)
+
     for copy in hot_copies:
         copy.wait_recv()
-    sums_out[...] = hot_all[...]
+    hot_copy = same(part_of(hot_all, core, 4 * piece), sibling)
+
+    for h in range(chunks):
+        for copy in third[h]:
+            copy.wait_recv()
+        part = part_2[h, z]
+        for k in range(depth - 1):
+            part += got_3[h, k]
+        top_out[:, h * chunk : (h + 1) * chunk] = part
     cold_copy.wait_recv()
     cold_out[...] = cold_full[...].reshape(cold_out.shape)
+    hot_copy.wait_recv()
+    sums_out[...] = hot_all[...]
     for copy in started:
         copy.wait_send()
 
@@ -355,48 +397,58 @@
     hot_rows = cache.shape[0]
     depth = n // 2
     rows = features // (4 * n)
-    half, chunk = columns // 2, columns // 4
+    chunk = columns // 4
     sum_rows = blocks.shape[0] * BLOCK + columns // width
     piece = -(-sum_rows // 64) * 8
     f32 = lambda *shape: pltpu.VMEM(shape, jnp.float32)
     b16 = lambda *shape: pltpu.VMEM(shape, jnp.bfloat16)
     i32 = lambda *shape: pltpu.VMEM(shape, jnp.int32)
-    copies = 4 * (n - 1) + 1 + 4 + 2 * (depth - 1 + 3) + 7 + depth - 1 + 7 + 3
+    copies = 6 * n + 8 * depth + 32
     vmem = pl.BlockSpec(memory_space=pltpu.VMEM)
-    hbm = pl.BlockSpec(memory_space=pl.ANY)
+    hbm = pl.BlockSpec(memory_space=pltpu.HBM)
     out = lambda *shape: jax.ShapeDtypeStruct(shape, jnp.float32)
     return pl.pallas_call(
         functools.partial(step_kernel, n, piece),
         out_shape=(
             out(rows, columns), out(8 * piece, width), out(own_rows, width), out(hot_rows, width)
         ),
-        in_specs=[vmem] * 5 + [pl.BlockSpec(memory_space=pltpu.SMEM)] + [hbm] * 4,
+        in_specs=[hbm] * 10,
         out_specs=(vmem,) * 4,
         scratch_shapes=[
-            b16(features, columns), f32(2, own_rows // 2, width), f32(hot_rows, width),
-            f32(hot_rows, width), b16(n, 2, own_rows // 2, width), i32(n, 1, cap), i32(n, 1, cap),
+            i32(hot_feats, samples), i32(1, lookups), i32(1, lookups), i32(1, samples),
+            f32(1, columns), pltpu.SMEM(blocks.shape, jnp.int32),
+            b16(features, columns), f32(4, own_rows // 4, width),
+            f32(4, own_rows // 4, width), f32(hot_rows, width),
+            f32(hot_rows, width), b16(n, 4, own_rows // 4, width), i32(n, 1, cap), i32(n, 1, cap),
             b16(n, lookups, own_rows), b16(n * cap, lookups), b16(hot_rows, hot_feats * samples),
             b16(own_rows, n * cap),
             f32(samples, columns), f32(samples, columns), b16(samples, columns),
             b16(4 * depth, 2, rows, samples), b16(4 * depth, rows, samples),
             b16(4, samples, chunk), b16(4, samples, chunk),
             b16(n, cap, width), b16(n, cap, width),
-            f32(depth, 4, rows, half), f32(depth, 4, rows, half),
-            f32(3, depth, rows, half), f32(depth - 1, 4, rows, half),
-            f32(depth, rows, half), f32(4, rows, half),
-            f32(depth - 1, rows, half), f32(3, rows, half),
+            f32(4, depth, 2, 2, rows, chunk), b16(4, depth, 2, rows, chunk),
+            b16(4, depth, 2, rows, chunk),
+            f32(4, depth, 2, rows, chunk), f32(4, depth, rows, chunk), f32(4, depth, rows, chunk),
+            f32(4, depth - 1, rows, chunk),
             f32(2, own_rows // 2, width), f32(own_rows // 2, width), f32(own_rows // 2, width),
             f32(own_rows // 2, width), f32(2, own_rows // 2, width),
-            f32(8 * piece, width), f32(7, piece, width), f32(depth, piece, width),
-            f32(8 * piece, width),
-            pltpu.SemaphoreType.DMA((4,)),
+            f32(8 * piece, width), f32(4 * piece, width), f32(4 * piece, width),
+            f32(3, piece, width), f32(depth, piece, width), f32(8 * piece, width),
+            pltpu.SemaphoreType.DMA((11,)),
             pltpu.SemaphoreType.DMA((copies,)),
             pltpu.SemaphoreType.DMA((copies,)),
         ],
-        compiler_params=pltpu.CompilerParams(collective_id=0, has_side_effects=True),
+        compiler_params=pltpu.CompilerParams(
+            collective_id=0, has_side_effects=True, vmem_limit_bytes=VMEM_LIMIT
+        ),
     )(
-        hot_ids, owner, offset, labels, out_weight, blocks,
-        weight, table.reshape(2, own_rows // 2, width), cache, pending,
+        *[
+            pltpu.with_memory_space_constraint(value, pltpu.HBM)
+            for value in (
+                hot_ids, owner, offset, labels, out_weight, blocks,
+                weight, table.reshape(4, own_rows // 4, width), cache, pending,
+            )
+        ]
     )
 
 
@@ -434,6 +486,7 @@
         ),
         in_specs=[smem] * 2 + [vmem] * 8,
         out_specs=(vmem,) * 7,
+        compiler_params=pltpu.CompilerParams(vmem_limit_bytes=VMEM_LIMIT // 2),
     )(blocks, clock, top, sums, cold, carried, table, accum, cache, hot_accum)
 
 

time: 56.2 us -> 45.4 us (0.81)
  Pallas kernels: 55.1 us -> 43.9 us
  local copies, waits for them, and re-layouts: 0 us -> 0.63 us
    pallas_call x1, Pallas kernels: 51.8 us -> 41.8 us  [step(): pl.pallas_call(functools.partial(step_kernel, n, piece), out_shape=(out(r...]
    pallas_call x1, Pallas kernels: 3.3 us -> 2.08 us  [update(): pl.pallas_call(update_kernel, out_shape=(like(table), like(accum), like(c...]
    unnamed x0 -> x12, local copies, waits for them, and re-layouts: none -> 0.63 us
where the time goes in v2:
time: 45.4 us; the launch traced here: 45.3 us
  Pallas kernels  43.9 us (97%)
  between operations  0.72 us (2%)
  local copies, waits for them, and re-layouts  0.63 us (1%)
    pallas_call x1, Pallas kernels, step(): pl.pallas_call(functools.partial(step_kernel, n, piece), out_shape=(out(r...  41.8 us
    pallas_call x1, Pallas kernels, update(): pl.pallas_call(update_kernel, out_shape=(like(table), like(accum), like(c...  2.08 us

profile of v2, /device:TPU:0, one launch (start us, length us, event | category | flops | bytes accessed | tf_op | source)
XLA Modules:
  0.0 45.3 jit_solution(7639381260962360185)
XLA Ops:
  0.6 0.0 copy-start
  0.6 0.0 copy-start.1
  0.7 0.0 copy-start.2
  0.7 0.0 copy-start.3
  0.7 41.8 %shard_map.180 = (f32[16,1024]{1,0:T(8,128)S(1)}, f32[448,128]{1,0:T(8,128)S(1)}, f32[512,128]{1,0:T(8,128)S(1)}, f32[1024,128]{1,0:T(8,128)S(1)}) custom-call(s32[2,256]{1,0:T(2,128)} %bitcast.9, s32[1,512]{1,0:T(1,128)} %bitcast.10, s32[1,512]{1,0:T(1,128)} %bitcast.11, s32[1,256]{1,0:T(1,128)} %bitcast.12, f32[1,1024]{1,0:T(1,128)} %bitcast.8, s32[3]{0:T(128)} %blocks.1, ...), custom_call_target="tpu_custom_call" | custom-call | tf_op jit(solution)/shard_map/pallas_call | solution.py:410
  42.5 0.0 copy-start.4
  42.5 0.0 copy-start.5
  42.6 0.0 copy-done
  42.6 0.0 copy-done.1
  42.6 0.0 copy-done.2
  42.6 0.0 copy-done.3
  42.6 0.6 %copy-done.4 = s32[3]{0:T(128)S(1)} copy-done((s32[3]{0:T(128)S(1)}, s32[3]{0:T(128)}, u32[]{:S(2)}) %copy-start.4) | copy-done | bytes 36
  43.2 0.0 copy-done.5
  43.2 2.1 %shard_map.181 = (f32[512,128]{1,0:T(8,128)}, f32[512,128]{1,0:T(8,128)}, f32[1024,128]{1,0:T(8,128)}, f32[1024,128]{1,0:T(8,128)}, f32[1024,128]{1,0:T(8,128)}, /*index=5*/f32[16,1024]{1,0:T(8,128)}, f32[8,128]{1,0:T(8,128)}) custom-call(s32[3]{0:T(128)S(1)} %copy-done.4, s32[8]{0:T(128)S(1)} %copy-done.5, f32[16,1024]{1,0:T(8,128)S(1)} %get-tuple-element.18.top, ...), custom_call_target="tpu_custom_call" | custom-call | tf_op jit(solution)/shard_map/pallas_call | solution.py:481
Async XLA Ops:
  0.6 41.9 %copy-start = (f32[1024,128]{1,0:T(8,128)S(1)}, f32[1024,128]{1,0:T(8,128)}, u32[]{:S(2)}) copy-start(f32[1024,128]{1,0:T(8,128)} %cache.3) | copy-start | bytes 1572868
  0.6 41.9 %copy-start.1 = (f32[512,128]{1,0:T(8,128)S(1)}, f32[512,128]{1,0:T(8,128)}, u32[]{:S(2)}) copy-start(f32[512,128]{1,0:T(8,128)} %table.1) | copy-start | bytes 786436
  0.7 41.9 %copy-start.2 = (f32[1024,128]{1,0:T(8,128)S(1)}, f32[1024,128]{1,0:T(8,128)}, u32[]{:S(2)}) copy-start(f32[1024,128]{1,0:T(8,128)} %hot_accum.1) | copy-start | bytes 1572868
  0.7 41.9 %copy-start.3 = (f32[512,128]{1,0:T(8,128)S(1)}, f32[512,128]{1,0:T(8,128)}, u32[]{:S(2)}) copy-start(f32[512,128]{1,0:T(8,128)} %accum.1) | copy-start | bytes 786436
  42.5 0.7 %copy-start.4 = (s32[3]{0:T(128)S(1)}, s32[3]{0:T(128)}, u32[]{:S(2)}) copy-start(s32[3]{0:T(128)} %blocks.1) | copy-start | bytes 40
  42.5 0.7 %copy-start.5 = (s32[8]{0:T(128)S(1)}, s32[8]{0:T(128)}, u32[]{:S(2)}) copy-start(s32[8]{0:T(128)} %clock.1) | copy-start | bytes 100

commit v3 on v2

--- a/solution.py
+++ b/solution.py
@@ -80,8 +80,15 @@
     def near(mask):
         return (z * 2 + flip(x, mask & 4), flip(y, mask & 2) * 2 + flip(core, mask & 1))
 
+    def level(k):
+        value = z
+        for weight in (1, 2, 4):
+            if k & weight:
+                value = value + weight * (1 - 2 * lax.rem(lax.div(z, weight), 2))
+        return value
+
     def along(k):
-        return lax.rem(z + k, depth) * 2 + x
+        return level(k) * 2 + x
 
     sibling, over_x, over_y = near(1), near(4), near(2)
     peers = [lax.rem(me + j, n) for j in range(1, n)]
@@ -92,13 +99,13 @@
         pl.semaphore_signal(barrier, inc=1, device_id=device, device_id_type=MESH)
     local = []
     for src, dst in [
-        (table.at[rep], table_v.at[rep]), (owner_in, owner), (offset_in, offset),
+        (table.at[rep], table_v), (owner_in, owner), (offset_in, offset),
         (table, table_all), (hot_ids_in, hot_ids), (cache, cache_v),
         (weight, weight_v), (labels_in, labels), (out_weight_in, out_weight), (blocks_in, blocks),
         (pending, pending_v),
     ]:
         local.append(pltpu.make_async_copy(src, dst, loads.at[len(local)]))
-        local[-1].start()
+    local[0].start()
 
     count = [0]
     started = []
@@ -115,11 +122,13 @@
         return send(ref, ref, device)
 
     local[0].wait()
-    tables[me, rep] = table_v[rep].astype(bf16)
+    tables[me, rep] = table_v[...].astype(bf16)
+    for copy in local[1:]:
+        copy.start()
     pl.semaphore_wait(barrier, len(greeted))
     mine = tables.at[me, rep]
-    order = sorted(range(1, depth), key=lambda k: abs(2 * k - depth))
-    z_table = {k: same(mine, (along(k), rep)) for k in order}
+    order = list(range(1, depth))
+    z_table = {k: same(mine, (along(k), rep)) for k in order[::-1]}
     x_table = same(mine, over_x)
 
     samples = hot_ids.shape[1]
@@ -170,13 +179,20 @@
     def looked(o):
         return matmul(look[o], tables[o].reshape(own_rows, width))
 
-    order = order[::-1]
     x_source = z * 2 + 1 - x
-    z_source = {k: lax.rem(z + depth - k, depth) * 2 + x for k in order}
-    far_source = {k: lax.rem(z + depth - k, depth) * 2 + 1 - x for k in order}
+    z_source = {k: along(k) for k in order}
+    far_source = {k: level(k) * 2 + 1 - x for k in order}
     others = [x_source] + [z_source[k] for k in order] + [far_source[k] for k in order]
     by_y, by_core, y_core, by_x = {}, {}, {}, {}
     by_y[0], by_core[0] = relay(x_table, x_source, over_y, sibling)
+
+    def relay_z(i):
+        k = order[i]
+        by_x[k], by_y[1 + i], by_core[1 + i] = relay(
+            z_table[k], z_source[k], over_x, over_y, sibling
+        )
+
+    relay_z(0)
 
     local[4].wait()
     hot_col = jnp.concatenate(
@@ -189,10 +205,8 @@
     )
     hot_x = [hot_found[k * samples : (k + 1) * samples] for k in range(hot_feats)]
 
-    for i, k in enumerate(order):
-        by_x[k], by_y[1 + i], by_core[1 + i] = relay(
-            z_table[k], z_source[k], over_x, over_y, sibling
-        )
+    for i in range(1, depth - 1):
+        relay_z(i)
 
     local[6].wait()
     hot_wide = jnp.concatenate(hot_x, axis=1).astype(bf16)
@@ -208,7 +222,6 @@
         y_core[i] = same(tables.at[others[i], (1 - y) * 2 + core], sibling)
 
     relay_y(0)
-    cold_found = looked(me)
     for i, k in enumerate(order):
         by_y[depth + i], by_core[depth + i] = relay(by_x[k], far_source[k], over_y, sibling)
         relay_y(1 + i)
@@ -219,16 +232,19 @@
         jnp.concatenate([hot_ids[k : k + 1] for k in range(hot_feats)], axis=1),
         (hot_rows, hot_feats * samples), 0,
     )
+    cold_found = looked(me)
+
+    def found(j):
+        by_core[j].wait_recv()
+        y_core[j].wait_recv()
+        return looked(others[j])
+
+    cold_found += found(0)
     for i in range(depth, n - 1):
         relay_y(i)
-        j = i - depth
-        by_core[j].wait_recv()
-        y_core[j].wait_recv()
-        cold_found += looked(others[j])
-    for j in range(depth - 1, n - 1):
-        by_core[j].wait_recv()
-        y_core[j].wait_recv()
-        cold_found += looked(others[j])
+        cold_found += found(i - depth + 1)
+    for j in range(depth, n - 1):
+        cold_found += found(j)
     cold_x = [cold_found[k * samples : (k + 1) * samples] for k in range(feats)]
     inputs_t[...] = (
         jnp.concatenate([part.T for part in hot_x + cold_x], axis=0)
@@ -256,20 +272,53 @@
         dh[h] = (errors * gate[:, at]).astype(bf16)
         dh_copies.append(send(dh.at[h], dh_got.at[h], sibling))
 
-    dinputs = matmul(dh[0], weight_v[:, :chunk], (1, 1))
-    for h in range(1, chunks):
-        dinputs += matmul(dh[h], weight_v[:, h * chunk : (h + 1) * chunk], (1, 1))
-    dinputs = dinputs.astype(bf16)
-    cold_dx = jnp.concatenate(
-        [dinputs[:, hot_in + k * width : hot_in + (k + 1) * width] for k in range(feats)], axis=0
-    )
+    def dinputs(rows):
+        total = matmul(dh[0], weight_v[rows, :chunk], (1, 1))
+        for h in range(1, chunks):
+            total += matmul(dh[h], weight_v[rows, h * chunk : (h + 1) * chunk], (1, 1))
+        total = total.astype(bf16)
+        return jnp.concatenate(
+            [total[:, k : k + width] for k in range(0, total.shape[1], width)], axis=0
+        )
+
+    cold_dx = dinputs(slice(hot_in, weight_v.shape[0]))
     outgoing[...] = matmul(placed_t[...], cold_dx).astype(bf16).reshape(outgoing.shape)
     cold_copies = [send(outgoing.at[peer], incoming.at[me], (peer, rep)) for peer in peers]
     incoming[me] = outgoing[me]
 
-    hot_dx = jnp.concatenate(
-        [dinputs[:, k * width : (k + 1) * width] for k in range(hot_feats)], axis=0
-    )
+    inputs_copy.wait_recv()
+
+    def x_first(h):
+        return h == chunks - 1
+
+    def first_step(h):
+        both = matmul(inputs_t[:, core].reshape(-1, samples), dh[h])
+        dh_copies[h].wait_recv()
+        both += matmul(inputs_got[...].reshape(-1, samples), dh_got[h])
+        top[h] = both.reshape(top.shape[1:])
+        leaving = top[h, :, 1 - x] if x_first(h) else top[h, :, :, 1 - y]
+        leave[h] = leaving.astype(bf16)
+        return send(leave.at[h], got_1.at[h], over_x if x_first(h) else over_y)
+
+    def second_step(h):
+        first[h].wait_recv()
+        kept = top[h, :, x] if x_first(h) else top[h, :, :, y]
+        part_1[h] = kept + got_1[h].astype(f32)
+        if x_first(h):
+            return send(part_1.at[h, :, 1 - y], got_2.at[h], over_y)
+        return send(part_1.at[h, :, 1 - x], got_2.at[h], over_x)
+
+    def third_step(h):
+        second[h].wait_recv()
+        part_2[h] = part_1[h, :, y if x_first(h) else x] + got_2[h]
+        return [
+            send(part_2.at[h, level(k)], got_3.at[h, k - 1], (along(k), rep))
+            for k in range(1, depth)
+        ]
+
+    first = [first_step(h) for h in range(chunks // 2)]
+
+    hot_dx = dinputs(slice(0, hot_in))
     local[9].wait()
     local[10].wait()
     carried_out[...] = pending_v[...] + matmul(hot_t[...], hot_dx)
@@ -298,39 +347,8 @@
     my_quad = x * 2 + y
     quads = [(flip(x, m & 4) * 2 + flip(y, m & 2), near(m)) for m in (2, 4, 6)]
 
-    inputs_copy.wait_recv()
-
-    def first_step(h):
-        both = matmul(inputs_t[:, core].reshape(-1, samples), dh[h])
-        dh_copies[h].wait_recv()
-        both += matmul(inputs_got[...].reshape(-1, samples), dh_got[h])
-        top[h] = both.reshape(top.shape[1:])
-        leaving = top[h, :, 1 - x] if h % 2 == 0 else top[h, :, :, 1 - y]
-        leave[h] = leaving.astype(bf16)
-        return send(leave.at[h], got_1.at[h], over_x if h % 2 == 0 else over_y)
-
-    def second_step(h):
-        first[h].wait_recv()
-        kept = top[h, :, x] if h % 2 == 0 else top[h, :, :, y]
-        part_1[h] = kept + got_1[h].astype(f32)
-        if h % 2 == 0:
-            return send(part_1.at[h, :, 1 - y], got_2.at[h], over_y)
-        return send(part_1.at[h, :, 1 - x], got_2.at[h], over_x)
-
-    def third_step(h):
-        second[h].wait_recv()
-        part_2[h] = part_1[h, :, y if h % 2 == 0 else x] + got_2[h]
-        return [
-            send(part_2.at[h, lax.rem(z + k, depth)], got_3.at[h, k - 1], (along(k), rep))
-            for k in range(1, depth)
-        ]
-
-    first = [first_step(h) for h in range(chunks)]
-
-    for o in range(n - 1):
-        asking[o].wait_recv()
-    for o in range(n):
-        own_hot[:, o * cap : (o + 1) * cap] = one_hot(asked[o], (own_rows, cap), 0)
+    first += [first_step(h) for h in range(chunks // 2, chunks)]
+
 
     hot_copy.wait_recv()
     hot_mid[...] = part_of(hot_sum, core, 4 * piece)[...] + hot_got[...]
@@ -338,6 +356,10 @@
         send(part_of(hot_mid, q, piece), hot_near.at[i], device)
         for i, (q, device) in enumerate(quads)
     ]
+    for o in range(n - 1):
+        asking[o].wait_recv()
+    for o in range(n):
+        own_hot[:, o * cap : (o + 1) * cap] = one_hot(asked[o], (own_rows, cap), 0)
 
     second = [second_step(h) for h in range(chunks)]
 
@@ -351,11 +373,11 @@
     cold[...] = matmul(own_hot[...], incoming[...].reshape(n * cap, width)).reshape(cold.shape)
     cold_copy = send(cold.at[1 - core], cold_got, sibling)
 
-    third = [third_step(h) for h in range(chunks)]
-
     cold_copy.wait_recv()
     cold_half[...] = cold[core] + cold_got[...]
     cold_copy = send(cold_half, cold_last, over_y)
+
+    third = [third_step(h) for h in range(chunks)]
 
     for copy in hot_copies:
         copy.wait_recv()
@@ -417,7 +439,7 @@
         scratch_shapes=[
             i32(hot_feats, samples), i32(1, lookups), i32(1, lookups), i32(1, samples),
             f32(1, columns), pltpu.SMEM(blocks.shape, jnp.int32),
-            b16(features, columns), f32(4, own_rows // 4, width),
+            b16(features, columns), f32(own_rows // 4, width),
             f32(4, own_rows // 4, width), f32(hot_rows, width),
             f32(hot_rows, width), b16(n, 4, own_rows // 4, width), i32(n, 1, cap), i32(n, 1, cap),
             b16(n, lookups, own_rows), b16(n * cap, lookups), b16(hot_rows, hot_feats * samples),
@@ -453,41 +475,74 @@
 
 
 def update_kernel(
-    blocks, clock, top, sums, cold, carried, table, accum, cache, hot_accum,
+    blocks_in, clock_in, top, sums, cold, carried, table, accum, cache, hot_accum,
     table_out, accum_out, cache_out, hot_accum_out, pending_out, top_out, head_out,
+    blocks, clock, table_next, accum_next, cache_next, hot_accum_next, pending_next, sems,
 ):
-    table_out[...], accum_out[...] = adagrad(table[...], accum[...], cold[...])
-    cache_out[...] = cache[...]
-    hot_accum_out[...] = hot_accum[...]
-    pending_out[...] = carried[...]
+    scalars = [
+        pltpu.make_async_copy(blocks_in, blocks, sems.at[0]),
+        pltpu.make_async_copy(clock_in, clock, sems.at[1]),
+    ]
+    for copy in scalars:
+        copy.start()
+    writes = []
+
+    def write(src, dst):
+        writes.append(pltpu.make_async_copy(src, dst, sems.at[2 + len(writes)]))
+        writes[-1].start()
+
     picks = blocks.shape[0]
+    write(top, top_out)
+    write(sums.at[picks * BLOCK : picks * BLOCK + head_out.shape[0]], head_out)
+    table_next[...], accum_next[...] = adagrad(table[...], accum[...], cold[...])
+    write(table_next, table_out)
+    write(accum_next, accum_out)
+    pending_next[...] = carried[...]
+    cache_next[...] = cache[...]
+    hot_accum_next[...] = hot_accum[...]
+    for copy in scalars:
+        copy.wait()
+    rows = [pl.ds(pl.multiple_of(blocks[k] * BLOCK, BLOCK), BLOCK) for k in range(picks)]
     for k in range(picks):
-        rows = pl.ds(pl.multiple_of(blocks[k] * BLOCK, BLOCK), BLOCK)
+        pending_next[rows[k], :] = jnp.zeros((BLOCK, cache.shape[1]), jnp.float32)
+    write(pending_next, pending_out)
+    for k in range(picks):
         divisor = 1.0 + clock[blocks[k]].astype(jnp.float32)
         flush = sums[k * BLOCK : (k + 1) * BLOCK, :] / divisor
-        cache_next, accum_next = adagrad(cache[rows, :], hot_accum[rows, :], flush)
-        cache_out[rows, :] = cache_next
-        hot_accum_out[rows, :] = accum_next
-        pending_out[rows, :] = jnp.zeros((BLOCK, cache.shape[1]), jnp.float32)
-    top_out[...] = top[...]
-    head_out[...] = sums[picks * BLOCK : picks * BLOCK + head_out.shape[0], :]
+        cache_next[rows[k], :], hot_accum_next[rows[k], :] = adagrad(
+            cache[rows[k], :], hot_accum[rows[k], :], flush
+        )
+    write(cache_next, cache_out)
+    write(hot_accum_next, hot_accum_out)
+    for copy in writes:
+        copy.wait()
 
 
 def update(blocks, clock, top, sums, cold, carried, table, accum, cache, hot_accum):
     head_rows = top.shape[1] // cache.shape[1]
-    smem = pl.BlockSpec(memory_space=pltpu.SMEM)
+    hbm = pl.BlockSpec(memory_space=pltpu.HBM)
     vmem = pl.BlockSpec(memory_space=pltpu.VMEM)
     like = lambda a: jax.ShapeDtypeStruct(a.shape, a.dtype)
+    scratch = lambda a: pltpu.VMEM(a.shape, a.dtype)
     return pl.pallas_call(
         update_kernel,
         out_shape=(
             like(table), like(accum), like(cache), like(hot_accum), like(carried), like(top),
             jax.ShapeDtypeStruct((head_rows, cache.shape[1]), jnp.float32),
         ),
-        in_specs=[smem] * 2 + [vmem] * 8,
-        out_specs=(vmem,) * 7,
+        in_specs=[hbm] * 2 + [vmem] * 8,
+        out_specs=(hbm,) * 7,
+        scratch_shapes=[
+            pltpu.SMEM(blocks.shape, jnp.int32), pltpu.SMEM(clock.shape, jnp.int32),
+            scratch(table), scratch(accum), scratch(cache), scratch(hot_accum), scratch(carried),
+            pltpu.SemaphoreType.DMA((9,)),
+        ],
         compiler_params=pltpu.CompilerParams(vmem_limit_bytes=VMEM_LIMIT // 2),
-    )(blocks, clock, top, sums, cold, carried, table, accum, cache, hot_accum)
+    )(
+        pltpu.with_memory_space_constraint(blocks, pltpu.HBM),
+        pltpu.with_memory_space_constraint(clock, pltpu.HBM),
+        top, sums, cold, carried, table, accum, cache, hot_accum,
+    )
 
 
 def suits(n, rep_n, top_weight, hot_ids, cold_offset, hot_cache, cold_table):
@@ -496,7 +551,7 @@
     return (
         rep_n == 4
         and n % 2 == 0
-        and 4 <= n <= 16
+        and n in (4, 8, 16)
         and features % (16 * 4 * n) == 0
         and columns % 1024 == 0
         and samples % 128 == 0

time: 45.4 us -> 43.9 us (0.967)
  Pallas kernels: 43.9 us -> 43 us
  local copies, waits for them, and re-layouts: 0.63 us -> 0.02 us
    pallas_call x1, Pallas kernels: 41.8 us -> 41.1 us  [step(): pl.pallas_call(functools.partial(step_kernel, n, piece), out_shape=(out(r...]
    unnamed x12 -> x8, local copies, waits for them, and re-layouts: 0.63 us -> 0.02 us
where the time goes in v3:
time: 43.9 us; the launch traced here: 43.7 us
  Pallas kernels  43 us (98%)
  between operations  0.71 us (2%)
    pallas_call x1, Pallas kernels, step(): pl.pallas_call(functools.partial(step_kernel, n, piece), out_shape=(out(r...  41.1 us
    pallas_call x1, Pallas kernels, update(): pl.pallas_call(update_kernel, out_shape=(like(table), like(accum), like(c...  1.92 us

profile of v3, /device:TPU:0, one launch (start us, length us, event | category | flops | bytes accessed | tf_op | source)
XLA Modules:
  0.0 43.7 jit_solution(9700038635079695211)
XLA Ops:
  0.6 0.0 copy-start
  0.6 0.0 copy-start.1
  0.7 0.0 copy-start.2
  0.7 0.0 copy-start.3
  0.7 41.1 %shard_map.180 = (f32[16,1024]{1,0:T(8,128)S(1)}, f32[448,128]{1,0:T(8,128)S(1)}, f32[512,128]{1,0:T(8,128)S(1)}, f32[1024,128]{1,0:T(8,128)S(1)}) custom-call(s32[2,256]{1,0:T(2,128)} %bitcast.9, s32[1,512]{1,0:T(1,128)} %bitcast.10, s32[1,512]{1,0:T(1,128)} %bitcast.11, s32[1,256]{1,0:T(1,128)} %bitcast.12, f32[1,1024]{1,0:T(1,128)} %bitcast.8, ...), custom_call_target="tpu_custom_call" | custom-call | tf_op jit(solution)/shard_map/pallas_call | solution.py:432
  41.8 0.0 copy-done
  41.8 0.0 copy-done.1
  41.8 0.0 copy-done.2
  41.8 0.0 copy-done.3
  41.8 1.9 %shard_map.181 = (f32[512,128]{1,0:T(8,128)}, f32[512,128]{1,0:T(8,128)}, f32[1024,128]{1,0:T(8,128)}, f32[1024,128]{1,0:T(8,128)}, f32[1024,128]{1,0:T(8,128)}, /*index=5*/f32[16,1024]{1,0:T(8,128)}, f32[8,128]{1,0:T(8,128)}) custom-call(s32[3]{0:T(128)} %blocks_in.3, s32[8]{0:T(128)} %clock_in.1, f32[16,1024]{1,0:T(8,128)S(1)} %get-tuple-element.18.top, ...), custom_call_target="tpu_custom_call" | custom-call | tf_op jit(solution)/shard_map/pallas_call | solution.py:527
Async XLA Ops:
  0.6 41.1 %copy-start = (f32[1024,128]{1,0:T(8,128)S(1)}, f32[1024,128]{1,0:T(8,128)}, u32[]{:S(2)}) copy-start(f32[1024,128]{1,0:T(8,128)} %cache.3) | copy-start | bytes 1572868
  0.6 41.1 %copy-start.1 = (f32[512,128]{1,0:T(8,128)S(1)}, f32[512,128]{1,0:T(8,128)}, u32[]{:S(2)}) copy-start(f32[512,128]{1,0:T(8,128)} %table.1) | copy-start | bytes 786436
  0.7 41.1 %copy-start.2 = (f32[1024,128]{1,0:T(8,128)S(1)}, f32[1024,128]{1,0:T(8,128)}, u32[]{:S(2)}) copy-start(f32[1024,128]{1,0:T(8,128)} %hot_accum.1) | copy-start | bytes 1572868
  0.7 41.1 %copy-start.3 = (f32[512,128]{1,0:T(8,128)S(1)}, f32[512,128]{1,0:T(8,128)}, u32[]{:S(2)}) copy-start(f32[512,128]{1,0:T(8,128)} %accum.1) | copy-start | bytes 786436

commit v4 on v3

--- a/solution.py
+++ b/solution.py
@@ -63,7 +63,7 @@
     hot_ids, owner, offset, labels, out_weight, blocks,
     weight_v, table_v, table_all, cache_v, pending_v, tables, requests, asked, look, placed_t, hot_t, own_hot,
     pre, gate, hidden, inputs_t, inputs_got, dh, dh_got, outgoing, incoming,
-    top, leave, got_1, part_1, got_2, part_2, got_3,
+    top, leave, got_1, part_1, got_2, part_2, got_3, leave_z, got_z, part_z, got_zx, part_zx, got_zy,
     cold, cold_got, cold_half, cold_last, cold_full, hot_sum, hot_got, hot_mid, hot_near, hot_z,
     hot_all,
     loads, sends, recvs,
@@ -105,7 +105,8 @@
         (pending, pending_v),
     ]:
         local.append(pltpu.make_async_copy(src, dst, loads.at[len(local)]))
-    local[0].start()
+    for copy in local[:3]:
+        copy.start()
 
     count = [0]
     started = []
@@ -123,7 +124,7 @@
 
     local[0].wait()
     tables[me, rep] = table_v[...].astype(bf16)
-    for copy in local[1:]:
+    for copy in local[3:]:
         copy.start()
     pl.semaphore_wait(barrier, len(greeted))
     mine = tables.at[me, rep]
@@ -168,10 +169,6 @@
     asking = [send(requests.at[peer], asked.at[me], (peer, rep)) for peer in peers]
     asked[me] = requests[me]
 
-    global_col = (owner_col * own_rows + offset_col).astype(jnp.int32)
-    for o in range(n):
-        look[o] = one_hot(global_col - o * own_rows, (lookups, own_rows), 1)
-
     def relay(copy, source, *devices):
         copy.wait_recv()
         return [same(tables.at[source, rep], device) for device in devices]
@@ -207,6 +204,10 @@
 
     for i in range(1, depth - 1):
         relay_z(i)
+
+    global_col = (owner_col * own_rows + offset_col).astype(jnp.int32)
+    for o in range(n):
+        look[o] = one_hot(global_col - o * own_rows, (lookups, own_rows), 1)
 
     local[6].wait()
     hot_wide = jnp.concatenate(hot_x, axis=1).astype(bf16)
@@ -288,33 +289,59 @@
 
     inputs_copy.wait_recv()
 
-    def x_first(h):
-        return h == chunks - 1
+    kinds = ["y", "y", "x", "z"]
 
     def first_step(h):
         both = matmul(inputs_t[:, core].reshape(-1, samples), dh[h])
         dh_copies[h].wait_recv()
         both += matmul(inputs_got[...].reshape(-1, samples), dh_got[h])
         top[h] = both.reshape(top.shape[1:])
-        leaving = top[h, :, 1 - x] if x_first(h) else top[h, :, :, 1 - y]
+        if kinds[h] == "z":
+            copies = []
+            for k in range(1, depth):
+                leave_z[k - 1] = top[h, level(k)].astype(bf16)
+                copies.append(send(leave_z.at[k - 1], got_z.at[k - 1], (along(k), rep)))
+            return copies
+        leaving = top[h, :, 1 - x] if kinds[h] == "x" else top[h, :, :, 1 - y]
         leave[h] = leaving.astype(bf16)
-        return send(leave.at[h], got_1.at[h], over_x if x_first(h) else over_y)
+        return [send(leave.at[h], got_1.at[h], over_x if kinds[h] == "x" else over_y)]
 
     def second_step(h):
-        first[h].wait_recv()
-        kept = top[h, :, x] if x_first(h) else top[h, :, :, y]
+        for copy in first[h]:
+            copy.wait_recv()
+        if kinds[h] == "z":
+            part = top[h, z]
+            for k in range(depth - 1):
+                part += got_z[k].astype(f32)
+            part_z[...] = part
+            return send(part_z.at[1 - x], got_zx, over_x)
+        kept = top[h, :, x] if kinds[h] == "x" else top[h, :, :, y]
         part_1[h] = kept + got_1[h].astype(f32)
-        if x_first(h):
+        if kinds[h] == "x":
             return send(part_1.at[h, :, 1 - y], got_2.at[h], over_y)
         return send(part_1.at[h, :, 1 - x], got_2.at[h], over_x)
 
     def third_step(h):
         second[h].wait_recv()
-        part_2[h] = part_1[h, :, y if x_first(h) else x] + got_2[h]
+        if kinds[h] == "z":
+            part_zx[...] = part_z[x] + got_zx[...]
+            return [send(part_zx.at[1 - y], got_zy, over_y)]
+        part_2[h] = part_1[h, :, y if kinds[h] == "x" else x] + got_2[h]
         return [
             send(part_2.at[h, level(k)], got_3.at[h, k - 1], (along(k), rep))
             for k in range(1, depth)
         ]
+
+    def last_step(h):
+        for copy in third[h]:
+            copy.wait_recv()
+        if kinds[h] == "z":
+            part = part_zx[y] + got_zy[...]
+        else:
+            part = part_2[h, z]
+            for k in range(depth - 1):
+                part += got_3[h, k]
+        top_out[:, h * chunk : (h + 1) * chunk] = part
 
     first = [first_step(h) for h in range(chunks // 2)]
 
@@ -361,7 +388,7 @@
     for o in range(n):
         own_hot[:, o * cap : (o + 1) * cap] = one_hot(asked[o], (own_rows, cap), 0)
 
-    second = [second_step(h) for h in range(chunks)]
+    second = {h: second_step(h) for h in (0, 1, 2)}
 
     for copy in hot_copies:
         copy.wait_recv()
@@ -373,11 +400,13 @@
     cold[...] = matmul(own_hot[...], incoming[...].reshape(n * cap, width)).reshape(cold.shape)
     cold_copy = send(cold.at[1 - core], cold_got, sibling)
 
+    second[3] = second_step(3)
+
     cold_copy.wait_recv()
     cold_half[...] = cold[core] + cold_got[...]
     cold_copy = send(cold_half, cold_last, over_y)
 
-    third = [third_step(h) for h in range(chunks)]
+    third = {h: third_step(h) for h in (2, 0, 1)}
 
     for copy in hot_copies:
         copy.wait_recv()
@@ -388,6 +417,8 @@
     part_of(hot_all, ours, piece)[...] = final
     hot_copies = [same(part_of(hot_all, ours, piece), device) for _, device in quads]
 
+    third[3] = third_step(3)
+
     cold_copy.wait_recv()
     cold_full[core] = cold_half[...] + cold_last[...]
     cold_copy = same(cold_full.at[core], sibling)
@@ -396,13 +427,8 @@
         copy.wait_recv()
     hot_copy = same(part_of(hot_all, core, 4 * piece), sibling)
 
-    for h in range(chunks):
-        for copy in third[h]:
-            copy.wait_recv()
-        part = part_2[h, z]
-        for k in range(depth - 1):
-            part += got_3[h, k]
-        top_out[:, h * chunk : (h + 1) * chunk] = part
+    for h in (3, 2, 0, 1):
+        last_step(h)
     cold_copy.wait_recv()
     cold_out[...] = cold_full[...].reshape(cold_out.shape)
     hot_copy.wait_recv()
@@ -451,7 +477,9 @@
             f32(4, depth, 2, 2, rows, chunk), b16(4, depth, 2, rows, chunk),
             b16(4, depth, 2, rows, chunk),
             f32(4, depth, 2, rows, chunk), f32(4, depth, rows, chunk), f32(4, depth, rows, chunk),
-            f32(4, depth - 1, rows, chunk),
+            f32(4, depth - 1, rows, chunk), b16(depth - 1, 2, 2, rows, chunk),
+            b16(depth - 1, 2, 2, rows, chunk), f32(2, 2, rows, chunk), f32(2, rows, chunk),
+            f32(2, rows, chunk), f32(rows, chunk),
             f32(2, own_rows // 2, width), f32(own_rows // 2, width), f32(own_rows // 2, width),
             f32(own_rows // 2, width), f32(2, own_rows // 2, width),
             f32(8 * piece, width), f32(4 * piece, width), f32(4 * piece, width),

time: 43.9 us -> 42.9 us (0.977)
  Pallas kernels: 43 us -> 42 us
    pallas_call x1, Pallas kernels: 41.1 us -> 40.1 us  [step(): pl.pallas_call(functools.partial(step_kernel, n, piece), out_shape=(out(r...]
where the time goes in v4:
time: 42.9 us; the launch traced here: 42.7 us
  Pallas kernels  42 us (98%)
  between operations  0.71 us (2%)
    pallas_call x1, Pallas kernels, step(): pl.pallas_call(functools.partial(step_kernel, n, piece), out_shape=(out(r...  40.1 us
    pallas_call x1, Pallas kernels, update(): pl.pallas_call(update_kernel, out_shape=(like(table), like(accum), like(c...  1.92 us

profile of v4, /device:TPU:0, one launch (start us, length us, event | category | flops | bytes accessed | tf_op | source)
XLA Modules:
  0.0 42.7 jit_solution(4758239925154417952)
XLA Ops:
  0.6 0.0 copy-start
  0.6 0.0 copy-start.1
  0.7 0.0 copy-start.2
  0.7 0.0 copy-start.3
  0.7 40.1 %shard_map.180 = (f32[16,1024]{1,0:T(8,128)S(1)}, f32[448,128]{1,0:T(8,128)S(1)}, f32[512,128]{1,0:T(8,128)S(1)}, f32[1024,128]{1,0:T(8,128)S(1)}) custom-call(s32[2,256]{1,0:T(2,128)} %bitcast.9, s32[1,512]{1,0:T(1,128)} %bitcast.10, s32[1,512]{1,0:T(1,128)} %bitcast.11, s32[1,256]{1,0:T(1,128)} %bitcast.12, f32[1,1024]{1,0:T(1,128)} %bitcast.8, ...), custom_call_target="tpu_custom_call" | custom-call | tf_op jit(solution)/shard_map/pallas_call | solution.py:458
  40.8 0.0 copy-done
  40.8 0.0 copy-done.1
  40.8 0.0 copy-done.2
  40.8 0.0 copy-done.3
  40.8 1.9 %shard_map.181 = (f32[512,128]{1,0:T(8,128)}, f32[512,128]{1,0:T(8,128)}, f32[1024,128]{1,0:T(8,128)}, f32[1024,128]{1,0:T(8,128)}, f32[1024,128]{1,0:T(8,128)}, /*index=5*/f32[16,1024]{1,0:T(8,128)}, f32[8,128]{1,0:T(8,128)}) custom-call(s32[3]{0:T(128)} %blocks_in.3, s32[8]{0:T(128)} %clock_in.1, f32[16,1024]{1,0:T(8,128)S(1)} %get-tuple-element.18.top, ...), custom_call_target="tpu_custom_call" | custom-call | tf_op jit(solution)/shard_map/pallas_call | solution.py:555
Async XLA Ops:
  0.6 40.1 %copy-start = (f32[1024,128]{1,0:T(8,128)S(1)}, f32[1024,128]{1,0:T(8,128)}, u32[]{:S(2)}) copy-start(f32[1024,128]{1,0:T(8,128)} %cache.3) | copy-start | bytes 1572868
  0.6 40.1 %copy-start.1 = (f32[512,128]{1,0:T(8,128)S(1)}, f32[512,128]{1,0:T(8,128)}, u32[]{:S(2)}) copy-start(f32[512,128]{1,0:T(8,128)} %table.1) | copy-start | bytes 786436
  0.7 40.1 %copy-start.2 = (f32[1024,128]{1,0:T(8,128)S(1)}, f32[1024,128]{1,0:T(8,128)}, u32[]{:S(2)}) copy-start(f32[1024,128]{1,0:T(8,128)} %hot_accum.1) | copy-start | bytes 1572868
  0.7 40.1 %copy-start.3 = (f32[512,128]{1,0:T(8,128)S(1)}, f32[512,128]{1,0:T(8,128)}, u32[]{:S(2)}) copy-start(f32[512,128]{1,0:T(8,128)} %accum.1) | copy-start | bytes 786436

commit v5 on v4

--- a/solution.py
+++ b/solution.py
@@ -90,10 +90,10 @@
     def along(k):
         return level(k) * 2 + x
 
-    sibling, over_x, over_y = near(1), near(4), near(2)
+    sibling, over_x, over_y, over_xy = near(1), near(4), near(2), near(6)
     peers = [lax.rem(me + j, n) for j in range(1, n)]
     sources = [lax.rem(me + n - j, n) for j in range(1, n)]
-    greeted = [(peer, rep) for peer in peers] + [sibling, over_y, near(6)]
+    greeted = [(peer, rep) for peer in peers] + [sibling, over_y, over_xy]
     barrier = pltpu.get_barrier_semaphore()
     for device in greeted:
         pl.semaphore_signal(barrier, inc=1, device_id=device, device_id_type=MESH)
@@ -131,6 +131,7 @@
     order = list(range(1, depth))
     z_table = {k: same(mine, (along(k), rep)) for k in order[::-1]}
     x_table = same(mine, over_x)
+    xy_table = same(mine, over_xy)
 
     samples = hot_ids.shape[1]
     hot_feats = hot_ids.shape[0]
@@ -181,12 +182,13 @@
     far_source = {k: level(k) * 2 + 1 - x for k in order}
     others = [x_source] + [z_source[k] for k in order] + [far_source[k] for k in order]
     by_y, by_core, y_core, by_x = {}, {}, {}, {}
-    by_y[0], by_core[0] = relay(x_table, x_source, over_y, sibling)
+    (by_core[0],) = relay(x_table, x_source, sibling)
+    by_y[0] = xy_table
 
     def relay_z(i):
         k = order[i]
-        by_x[k], by_y[1 + i], by_core[1 + i] = relay(
-            z_table[k], z_source[k], over_x, over_y, sibling
+        by_x[k], by_y[depth + i], by_y[1 + i], by_core[1 + i] = relay(
+            z_table[k], z_source[k], over_x, over_xy, over_y, sibling
         )
 
     relay_z(0)
@@ -222,29 +224,32 @@
         by_y[i].wait_recv()
         y_core[i] = same(tables.at[others[i], (1 - y) * 2 + core], sibling)
 
-    relay_y(0)
-    for i, k in enumerate(order):
-        by_y[depth + i], by_core[depth + i] = relay(by_x[k], far_source[k], over_y, sibling)
-        relay_y(1 + i)
-    placed_t[...] = one_hot(
-        col_to_row(target).astype(jnp.int32), (n * cap, lookups), 0
-    )
-    hot_t[...] = one_hot(
-        jnp.concatenate([hot_ids[k : k + 1] for k in range(hot_feats)], axis=1),
-        (hot_rows, hot_feats * samples), 0,
-    )
-    cold_found = looked(me)
-
     def found(j):
         by_core[j].wait_recv()
         y_core[j].wait_recv()
         return looked(others[j])
 
-    cold_found += found(0)
-    for i in range(depth, n - 1):
-        relay_y(i)
-        cold_found += found(i - depth + 1)
-    for j in range(depth, n - 1):
+    def relay_far(i):
+        k = order[i]
+        (by_core[depth + i],) = relay(by_x[k], far_source[k], sibling)
+        relay_y(1 + i)
+        relay_y(depth + i)
+
+    relay_y(0)
+    relay_far(0)
+    placed_t[...] = one_hot(
+        col_to_row(target).astype(jnp.int32), (n * cap, lookups), 0
+    )
+    hot_t[...] = one_hot(
+        jnp.concatenate([hot_ids[k : k + 1] for k in range(hot_feats)], axis=1),
+        (hot_rows, hot_feats * samples), 0,
+    )
+    cold_found = looked(me) + found(0)
+    for i in range(1, depth - 1):
+        relay_far(i)
+        if i < depth - 2:
+            cold_found += found(i)
+    for j in range(max(1, depth - 2), n - 1):
         cold_found += found(j)
     cold_x = [cold_found[k * samples : (k + 1) * samples] for k in range(feats)]
     inputs_t[...] = (
@@ -377,17 +382,19 @@
     first += [first_step(h) for h in range(chunks // 2, chunks)]
 
 
+    for o in range(n - 1):
+        asking[o].wait_recv()
+    for o in range(n):
+        own_hot[:, :, o * cap : (o + 1) * cap] = one_hot(asked[o], (own_rows, cap), 0).reshape(
+            2, own_rows // 2, cap
+        )
+
     hot_copy.wait_recv()
     hot_mid[...] = part_of(hot_sum, core, 4 * piece)[...] + hot_got[...]
     hot_copies = [
         send(part_of(hot_mid, q, piece), hot_near.at[i], device)
         for i, (q, device) in enumerate(quads)
     ]
-    for o in range(n - 1):
-        asking[o].wait_recv()
-    for o in range(n):
-        own_hot[:, o * cap : (o + 1) * cap] = one_hot(asked[o], (own_rows, cap), 0)
-
     second = {h: second_step(h) for h in (0, 1, 2)}
 
     for copy in hot_copies:
@@ -397,8 +404,10 @@
 
     for copy in cold_copies:
         copy.wait_recv()
-    cold[...] = matmul(own_hot[...], incoming[...].reshape(n * cap, width)).reshape(cold.shape)
+    arrived = incoming[...].reshape(n * cap, width)
+    cold[1 - core] = matmul(own_hot[1 - core], arrived)
     cold_copy = send(cold.at[1 - core], cold_got, sibling)
+    cold[core] = matmul(own_hot[core], arrived)
 
     second[3] = second_step(3)
 
@@ -469,7 +478,7 @@
             f32(4, own_rows // 4, width), f32(hot_rows, width),
             f32(hot_rows, width), b16(n, 4, own_rows // 4, width), i32(n, 1, cap), i32(n, 1, cap),
             b16(n, lookups, own_rows), b16(n * cap, lookups), b16(hot_rows, hot_feats * samples),
-            b16(own_rows, n * cap),
+            b16(2, own_rows // 2, n * cap),
             f32(samples, columns), f32(samples, columns), b16(samples, columns),
             b16(4 * depth, 2, rows, samples), b16(4 * depth, rows, samples),
             b16(4, samples, chunk), b16(4, samples, chunk),

time: 42.9 us -> 41.9 us (0.977)
  Pallas kernels: 42 us -> 41 us
    pallas_call x1, Pallas kernels: 40.1 us -> 39.1 us  [step(): pl.pallas_call(functools.partial(step_kernel, n, piece), out_shape=(out(r...]
where the time goes in v5:
time: 41.9 us; the launch traced here: 41.7 us
  Pallas kernels  41 us (98%)
  between operations  0.71 us (2%)
    pallas_call x1, Pallas kernels, step(): pl.pallas_call(functools.partial(step_kernel, n, piece), out_shape=(out(r...  39.1 us
    pallas_call x1, Pallas kernels, update(): pl.pallas_call(update_kernel, out_shape=(like(table), like(accum), like(c...  1.92 us

profile of v5, /device:TPU:0, one launch (start us, length us, event | category | flops | bytes accessed | tf_op | source)
XLA Modules:
  0.0 41.7 jit_solution(8194246147968533752)
XLA Ops:
  0.6 0.0 copy-start
  0.6 0.0 copy-start.1
  0.7 0.0 copy-start.2
  0.7 0.0 copy-start.3
  0.7 39.1 %shard_map.180 = (f32[16,1024]{1,0:T(8,128)S(1)}, f32[448,128]{1,0:T(8,128)S(1)}, f32[512,128]{1,0:T(8,128)S(1)}, f32[1024,128]{1,0:T(8,128)S(1)}) custom-call(s32[2,256]{1,0:T(2,128)} %bitcast.9, s32[1,512]{1,0:T(1,128)} %bitcast.10, s32[1,512]{1,0:T(1,128)} %bitcast.11, s32[1,256]{1,0:T(1,128)} %bitcast.12, f32[1,1024]{1,0:T(1,128)} %bitcast.8, ...), custom_call_target="tpu_custom_call" | custom-call | tf_op jit(solution)/shard_map/pallas_call | solution.py:467
  39.8 0.0 copy-done
  39.8 0.0 copy-done.1
  39.8 0.0 copy-done.2
  39.8 0.0 copy-done.3
  39.8 1.9 %shard_map.181 = (f32[512,128]{1,0:T(8,128)}, f32[512,128]{1,0:T(8,128)}, f32[1024,128]{1,0:T(8,128)}, f32[1024,128]{1,0:T(8,128)}, f32[1024,128]{1,0:T(8,128)}, /*index=5*/f32[16,1024]{1,0:T(8,128)}, f32[8,128]{1,0:T(8,128)}) custom-call(s32[3]{0:T(128)} %blocks_in.3, s32[8]{0:T(128)} %clock_in.1, f32[16,1024]{1,0:T(8,128)S(1)} %get-tuple-element.18.top, ...), custom_call_target="tpu_custom_call" | custom-call | tf_op jit(solution)/shard_map/pallas_call | solution.py:564
Async XLA Ops:
  0.6 39.1 %copy-start = (f32[1024,128]{1,0:T(8,128)S(1)}, f32[1024,128]{1,0:T(8,128)}, u32[]{:S(2)}) copy-start(f32[1024,128]{1,0:T(8,128)} %cache.3) | copy-start | bytes 1572868
  0.6 39.1 %copy-start.1 = (f32[512,128]{1,0:T(8,128)S(1)}, f32[512,128]{1,0:T(8,128)}, u32[]{:S(2)}) copy-start(f32[512,128]{1,0:T(8,128)} %table.1) | copy-start | bytes 786436
  0.7 39.1 %copy-start.2 = (f32[1024,128]{1,0:T(8,128)S(1)}, f32[1024,128]{1,0:T(8,128)}, u32[]{:S(2)}) copy-start(f32[1024,128]{1,0:T(8,128)} %hot_accum.1) | copy-start | bytes 1572868
  0.7 39.1 %copy-start.3 = (f32[512,128]{1,0:T(8,128)S(1)}, f32[512,128]{1,0:T(8,128)}, u32[]{:S(2)}) copy-start(f32[512,128]{1,0:T(8,128)} %accum.1) | copy-start | bytes 786436

commit v6 on v5

--- a/solution.py
+++ b/solution.py
@@ -235,8 +235,6 @@
         relay_y(1 + i)
         relay_y(depth + i)
 
-    relay_y(0)
-    relay_far(0)
     placed_t[...] = one_hot(
         col_to_row(target).astype(jnp.int32), (n * cap, lookups), 0
     )
@@ -244,7 +242,10 @@
         jnp.concatenate([hot_ids[k : k + 1] for k in range(hot_feats)], axis=1),
         (hot_rows, hot_feats * samples), 0,
     )
-    cold_found = looked(me) + found(0)
+    cold_found = looked(me)
+    relay_y(0)
+    relay_far(0)
+    cold_found += found(0)
     for i in range(1, depth - 1):
         relay_far(i)
         if i < depth - 2:
@@ -291,64 +292,6 @@
     outgoing[...] = matmul(placed_t[...], cold_dx).astype(bf16).reshape(outgoing.shape)
     cold_copies = [send(outgoing.at[peer], incoming.at[me], (peer, rep)) for peer in peers]
     incoming[me] = outgoing[me]
-
-    inputs_copy.wait_recv()
-
-    kinds = ["y", "y", "x", "z"]
-
-    def first_step(h):
-        both = matmul(inputs_t[:, core].reshape(-1, samples), dh[h])
-        dh_copies[h].wait_recv()
-        both += matmul(inputs_got[...].reshape(-1, samples), dh_got[h])
-        top[h] = both.reshape(top.shape[1:])
-        if kinds[h] == "z":
-            copies = []
-            for k in range(1, depth):
-                leave_z[k - 1] = top[h, level(k)].astype(bf16)
-                copies.append(send(leave_z.at[k - 1], got_z.at[k - 1], (along(k), rep)))
-            return copies
-        leaving = top[h, :, 1 - x] if kinds[h] == "x" else top[h, :, :, 1 - y]
-        leave[h] = leaving.astype(bf16)
-        return [send(leave.at[h], got_1.at[h], over_x if kinds[h] == "x" else over_y)]
-
-    def second_step(h):
-        for copy in first[h]:
-            copy.wait_recv()
-        if kinds[h] == "z":
-            part = top[h, z]
-            for k in range(depth - 1):
-                part += got_z[k].astype(f32)
-            part_z[...] = part
-            return send(part_z.at[1 - x], got_zx, over_x)
-        kept = top[h, :, x] if kinds[h] == "x" else top[h, :, :, y]
-        part_1[h] = kept + got_1[h].astype(f32)
-        if kinds[h] == "x":
-            return send(part_1.at[h, :, 1 - y], got_2.at[h], over_y)
-        return send(part_1.at[h, :, 1 - x], got_2.at[h], over_x)
-
-    def third_step(h):
-        second[h].wait_recv()
-        if kinds[h] == "z":
-            part_zx[...] = part_z[x] + got_zx[...]
-            return [send(part_zx.at[1 - y], got_zy, over_y)]
-        part_2[h] = part_1[h, :, y if kinds[h] == "x" else x] + got_2[h]
-        return [
-            send(part_2.at[h, level(k)], got_3.at[h, k - 1], (along(k), rep))
-            for k in range(1, depth)
-        ]
-
-    def last_step(h):
-        for copy in third[h]:
-            copy.wait_recv()
-        if kinds[h] == "z":
-            part = part_zx[y] + got_zy[...]
-        else:
-            part = part_2[h, z]
-            for k in range(depth - 1):
-                part += got_3[h, k]
-        top_out[:, h * chunk : (h + 1) * chunk] = part
-
-    first = [first_step(h) for h in range(chunks // 2)]
 
     hot_dx = dinputs(slice(0, hot_in))
     local[9].wait()
@@ -379,6 +322,70 @@
     my_quad = x * 2 + y
     quads = [(flip(x, m & 4) * 2 + flip(y, m & 2), near(m)) for m in (2, 4, 6)]
 
+    inputs_copy.wait_recv()
+
+    kinds = ["y", "y", "x", "z"]
+
+    def first_step(h):
+        both = matmul(inputs_t[:, core].reshape(-1, samples), dh[h])
+        dh_copies[h].wait_recv()
+        both += matmul(inputs_got[...].reshape(-1, samples), dh_got[h])
+        top[h] = both.reshape(top.shape[1:])
+        if kinds[h] == "z":
+            copies = []
+            for k in range(1, depth):
+                leave_z[k - 1] = top[h, level(k)].astype(bf16)
+                copies.append(send(leave_z.at[k - 1], got_z.at[k - 1], (along(k), rep)))
+            return copies
+        leaving = top[h, :, 1 - x] if kinds[h] == "x" else top[h, :, :, 1 - y]
+        leave[h] = leaving.astype(bf16)
+        return [send(leave.at[h], got_1.at[h], over_x if kinds[h] == "x" else over_y)]
+
+    def second_step(h):
+        for copy in first[h]:
+            copy.wait_recv()
+        if kinds[h] == "z":
+            part = top[h, z]
+            for k in range(depth - 1):
+                part += got_z[k].astype(f32)
+            part_z[...] = part
+            return send(part_z.at[1 - x], got_zx, over_x)
+        kept = top[h, :, x] if kinds[h] == "x" else top[h, :, :, y]
+        part_1[h] = kept + got_1[h].astype(f32)
+        if kinds[h] == "x":
+            return send(part_1.at[h, :, 1 - y], got_2.at[h], over_y)
+        return send(part_1.at[h, :, 1 - x], got_2.at[h], over_x)
+
+    def third_step(h):
+        second[h].wait_recv()
+        if kinds[h] == "z":
+            part_zx[...] = part_z[x] + got_zx[...]
+            return [send(part_zx.at[1 - y], got_zy, over_y)]
+        part_2[h] = part_1[h, :, y if kinds[h] == "x" else x] + got_2[h]
+        return [
+            send(part_2.at[h, level(k)], got_3.at[h, k - 1], (along(k), rep))
+            for k in range(1, depth)
+        ]
+
+    def last_step(h):
+        for copy in third[h]:
+            copy.wait_recv()
+        if kinds[h] == "z":
+            part = part_zx[y] + got_zy[...]
+        else:
+            part = part_2[h, z]
+            for k in range(depth - 1):
+                part += got_3[h, k]
+        top_out[:, h * chunk : (h + 1) * chunk] = part
+
+    first = [first_step(h) for h in range(chunks // 2)]
+
+    hot_copy.wait_recv()
+    hot_mid[...] = part_of(hot_sum, core, 4 * piece)[...] + hot_got[...]
+    hot_copies = [
+        send(part_of(hot_mid, q, piece), hot_near.at[i], device)
+        for i, (q, device) in enumerate(quads)
+    ]
     first += [first_step(h) for h in range(chunks // 2, chunks)]
 
 
@@ -389,12 +396,6 @@
             2, own_rows // 2, cap
         )
 
-    hot_copy.wait_recv()
-    hot_mid[...] = part_of(hot_sum, core, 4 * piece)[...] + hot_got[...]
-    hot_copies = [
-        send(part_of(hot_mid, q, piece), hot_near.at[i], device)
-        for i, (q, device) in enumerate(quads)
-    ]
     second = {h: second_step(h) for h in (0, 1, 2)}
 
     for copy in hot_copies:

time: 41.9 us -> 41.9 us (level)
  no operation moved by 1% of the time
where the time goes in v6:
time: 41.9 us; the launch traced here: 41.7 us
  Pallas kernels  41 us (98%)
  between operations  0.71 us (2%)
    pallas_call x1, Pallas kernels, step(): pl.pallas_call(functools.partial(step_kernel, n, piece), out_shape=(out(r...  39.1 us
    pallas_call x1, Pallas kernels, update(): pl.pallas_call(update_kernel, out_shape=(like(table), like(accum), like(c...  1.92 us

profile of v6, /device:TPU:0, one launch (start us, length us, event | category | flops | bytes accessed | tf_op | source)
XLA Modules:
  0.0 41.7 jit_solution(10192432508235162248)
XLA Ops:
  0.6 0.0 copy-start
  0.6 0.0 copy-start.1
  0.7 0.0 copy-start.2
  0.7 0.0 copy-start.3
  0.7 39.1 %shard_map.180 = (f32[16,1024]{1,0:T(8,128)S(1)}, f32[448,128]{1,0:T(8,128)S(1)}, f32[512,128]{1,0:T(8,128)S(1)}, f32[1024,128]{1,0:T(8,128)S(1)}) custom-call(s32[2,256]{1,0:T(2,128)} %bitcast.9, s32[1,512]{1,0:T(1,128)} %bitcast.10, s32[1,512]{1,0:T(1,128)} %bitcast.11, s32[1,256]{1,0:T(1,128)} %bitcast.12, f32[1,1024]{1,0:T(1,128)} %bitcast.8, ...), custom_call_target="tpu_custom_call" | custom-call | tf_op jit(solution)/shard_map/pallas_call | solution.py:468
  39.8 0.0 copy-done
  39.8 0.0 copy-done.1
  39.8 0.0 copy-done.2
  39.8 0.0 copy-done.3
  39.8 1.9 %shard_map.181 = (f32[512,128]{1,0:T(8,128)}, f32[512,128]{1,0:T(8,128)}, f32[1024,128]{1,0:T(8,128)}, f32[1024,128]{1,0:T(8,128)}, f32[1024,128]{1,0:T(8,128)}, /*index=5*/f32[16,1024]{1,0:T(8,128)}, f32[8,128]{1,0:T(8,128)}) custom-call(s32[3]{0:T(128)} %blocks_in.3, s32[8]{0:T(128)} %clock_in.1, f32[16,1024]{1,0:T(8,128)S(1)} %get-tuple-element.18.top, ...), custom_call_target="tpu_custom_call" | custom-call | tf_op jit(solution)/shard_map/pallas_call | solution.py:565
Async XLA Ops:
  0.6 39.2 %copy-start = (f32[1024,128]{1,0:T(8,128)S(1)}, f32[1024,128]{1,0:T(8,128)}, u32[]{:S(2)}) copy-start(f32[1024,128]{1,0:T(8,128)} %cache.3) | copy-start | bytes 1572868
  0.6 39.2 %copy-start.1 = (f32[512,128]{1,0:T(8,128)S(1)}, f32[512,128]{1,0:T(8,128)}, u32[]{:S(2)}) copy-start(f32[512,128]{1,0:T(8,128)} %table.1) | copy-start | bytes 786436
  0.7 39.2 %copy-start.2 = (f32[1024,128]{1,0:T(8,128)S(1)}, f32[1024,128]{1,0:T(8,128)}, u32[]{:S(2)}) copy-start(f32[1024,128]{1,0:T(8,128)} %hot_accum.1) | copy-start | bytes 1572868
  0.7 39.2 %copy-start.3 = (f32[512,128]{1,0:T(8,128)S(1)}, f32[512,128]{1,0:T(8,128)}, u32[]{:S(2)}) copy-start(f32[512,128]{1,0:T(8,128)} %accum.1) | copy-start | bytes 786436
